TPU v7x, 16 devices: a 4x2x1 block of a 4x4x8 slice. The times are simulated.
16 devices in a mesh: dp: 2 (over y, z), ep: 8 (over x, core).
Axes of the slice: x: 4, y: 2, z: 1, core: 2. Of those that a mesh axis runs over, the one named last changes fastest.
The devices are a block of a 4x4x8 slice.
Arguments:
- tok_in: bfloat16 [2048, 2048], P(('dp', 'ep')), parts along dimension 0
- lat_cache: bfloat16 [2048, 64, 512], P(('dp', 'ep')), parts along dimension 0
- rope_cache: bfloat16 [2048, 64, 64], P(('dp', 'ep')), parts along dimension 0
- tok_pos: int32 [2048], P(('dp', 'ep')), parts along dimension 0
- expert_ids: int32 [2048, 6], P(('dp', 'ep')), parts along dimension 0
- attn_gain: bfloat16 [2048], replicated
- w_query: bfloat16 [2048, 3072], replicated
- w_kvdown: bfloat16 [2048, 576], replicated
- w_ukey: bfloat16 [16, 128, 512], replicated
- w_uval: bfloat16 [16, 512, 128], replicated
- w_out: bfloat16 [2048, 2048], replicated
- ffn_gain: bfloat16 [2048], replicated
- w_router: bfloat16 [2048, 64], replicated
- sh_gate: bfloat16 [2048, 2816], replicated
- sh_up: bfloat16 [2048, 2816], replicated
- sh_down: bfloat16 [2816, 2048], replicated
- ex_gate: bfloat16 [64, 2048, 1408], P('ep')
- ex_up: bfloat16 [64, 2048, 1408], P('ep')
- ex_down: bfloat16 [64, 1408, 2048], P('ep')
Outputs:
- output 1: bfloat16 [2048, 2048], P(('dp', 'ep')), parts along dimension 0
- output 2: bfloat16 [2048, 64, 512], P(('dp', 'ep')), parts along dimension 0
- output 3: bfloat16 [2048, 64, 64], P(('dp', 'ep')), parts along dimension 0
There are 2 independent parts. A program takes and returns all parts, laid end to end along the dimension named above; an argument that names none is the same for every part.
All inputs are finite; a program needn't handle non-finite values.
Results may differ from a plain program's by a relative error of at most 0.0130158.
Values are sent between devices in bfloat16 or wider.
A program may use at most 768 MiB of HBM per device.

v0:
```python
import jax
import jax.numpy as jnp
from jax import lax
from jax.sharding import PartitionSpec as P

ROUTE_SCALE = 2.827
ROPE_BASE = 10000.0
NORM_EPS = 1e-6


def unit_norm(values):
    mean_sq = jnp.mean(jnp.square(values), axis=-1, keepdims=True)
    return values * lax.rsqrt(mean_sq + NORM_EPS)


def rms_norm(values, gain_vec):
    return unit_norm(values) * gain_vec.astype(jnp.float32)


def rope_rotate(values, angle_rad):
    half_dim = values.shape[-1] // 2
    x_first = values[..., :half_dim]
    x_second = values[..., half_dim:]
    cos_part = jnp.cos(angle_rad)
    sin_part = jnp.sin(angle_rad)
    return jnp.concatenate([x_first * cos_part - x_second * sin_part, x_second * cos_part + x_first * sin_part], axis=-1)


def attention_block(tok_in, lat_cache, rope_cache, tok_pos, attn_gain, w_query, w_kvdown, w_ukey, w_uval, w_out, ffn_gain):
    num_heads, nope_dim, kv_rank = w_ukey.shape
    rope_dim = rope_cache.shape[-1]
    seq_len = lat_cache.shape[1]
    tok_rows = tok_in.shape[0]
    x_wide = tok_in.astype(jnp.float32)
    x_norm = rms_norm(x_wide, attn_gain).astype(jnp.bfloat16)
    q_all = jnp.dot(x_norm, w_query, preferred_element_type=jnp.float32).astype(jnp.bfloat16).reshape(tok_rows, num_heads, nope_dim + rope_dim)
    kv_all = jnp.dot(x_norm, w_kvdown, preferred_element_type=jnp.float32)
    inv_freq = ROPE_BASE ** (-(2.0 * jnp.arange(rope_dim // 2)) / rope_dim)
    angle_rad = tok_pos.astype(jnp.float32)[:, None] * inv_freq[None, :]
    lat_new = unit_norm(kv_all[:, :kv_rank]).astype(jnp.bfloat16)
    rope_new = rope_rotate(kv_all[:, kv_rank:], angle_rad).astype(jnp.bfloat16)
    q_rope = rope_rotate(q_all[:, :, nope_dim:].astype(jnp.float32), angle_rad[:, None, :]).astype(jnp.bfloat16)
    q_lat = jnp.einsum('bhn,hnc->bhc', q_all[:, :, :nope_dim], w_ukey, preferred_element_type=jnp.float32).astype(jnp.bfloat16)
    seq_ids = jnp.arange(seq_len)
    at_pos = (seq_ids[None, :] == tok_pos[:, None])[:, :, None]
    lat_out = jnp.where(at_pos, lat_new[:, None, :], lat_cache)
    rope_out = jnp.where(at_pos, rope_new[:, None, :], rope_cache)
    scores = jnp.einsum('bhc,bsc->bhs', q_lat, lat_out, preferred_element_type=jnp.float32)
    scores = scores + jnp.einsum('bhr,bsr->bhs', q_rope, rope_out, preferred_element_type=jnp.float32)
    scores = scores * (nope_dim + rope_dim) ** -0.5
    visible = (seq_ids[None, :] <= tok_pos[:, None])[:, None, :]
    scores = jnp.where(visible, scores, -jnp.inf)
    prob_mat = jax.nn.softmax(scores, axis=-1).astype(jnp.bfloat16)
    o_lat = jnp.einsum('bhs,bsc->bhc', prob_mat, lat_out, preferred_element_type=jnp.float32).astype(jnp.bfloat16)
    o_heads = jnp.einsum('bhc,hcv->bhv', o_lat, w_uval, preferred_element_type=jnp.float32).astype(jnp.bfloat16)
    attn_out = jnp.dot(o_heads.reshape(tok_rows, -1), w_out, preferred_element_type=jnp.float32)
    resid_bf = (x_wide + attn_out).astype(jnp.bfloat16)
    h_norm = rms_norm(resid_bf.astype(jnp.float32), ffn_gain).astype(jnp.bfloat16)
    return resid_bf, h_norm, lat_out, rope_out


def route_weights(h_norm, w_router, expert_ids):
    num_experts = w_router.shape[1]
    gate_prob = jax.nn.sigmoid(jnp.dot(h_norm, w_router, preferred_element_type=jnp.float32))
    pick_mask = expert_ids[:, :, None] == jnp.arange(num_experts)[None, None, :]
    chosen = jnp.sum(jnp.where(pick_mask, gate_prob[:, None, :], 0.0), axis=-1)
    route_w = ROUTE_SCALE * chosen / jnp.sum(chosen, axis=1, keepdims=True)
    return route_w, pick_mask


def swiglu_shared(h_norm, sh_gate, sh_up, sh_down):
    gate_val = jnp.dot(h_norm, sh_gate, preferred_element_type=jnp.float32)
    up_val = jnp.dot(h_norm, sh_up, preferred_element_type=jnp.float32)
    act_val = (jax.nn.silu(gate_val) * up_val).astype(jnp.bfloat16)
    return jnp.dot(act_val, sh_down, preferred_element_type=jnp.float32)


def solution(mesh):
    ep_size = mesh.shape['ep']
    row_one = P(('dp', 'ep'))
    row_two = P(('dp', 'ep'), None)
    row_three = P(('dp', 'ep'), None, None)
    rep_one = P(None)
    rep_two = P(None, None)
    rep_three = P(None, None, None)
    exp_spec = P('ep', None, None)

    def local_step(tok_in, lat_cache, rope_cache, tok_pos, expert_ids, attn_gain, w_query, w_kvdown, w_ukey, w_uval, w_out, ffn_gain, w_router, sh_gate, sh_up, sh_down, ex_gate, ex_up, ex_down):
        resid_bf, h_norm, lat_out, rope_out = attention_block(tok_in, lat_cache, rope_cache, tok_pos, attn_gain, w_query, w_kvdown, w_ukey, w_uval, w_out, ffn_gain)
        route_w, pick_mask = route_weights(h_norm, w_router, expert_ids)
        shared_out = swiglu_shared(h_norm, sh_gate, sh_up, sh_down)
        tok_rows, top_k = expert_ids.shape
        num_experts = w_router.shape[1]
        local_experts = ex_gate.shape[0]
        d_model = h_norm.shape[1]
        cap_slots = max(2, -(-2 * tok_rows * top_k // num_experts))
        pick_int = pick_mask.astype(jnp.int32)
        per_tok = jnp.sum(pick_int, axis=1)
        before = jnp.cumsum(per_tok, axis=0) - per_tok
        slot_idx = jnp.sum(pick_int * before[:, None, :], axis=-1)
        slot_hot = slot_idx[:, :, None] == jnp.arange(cap_slots)
        place_hot = (pick_mask[:, :, :, None] & slot_hot[:, :, None, :]).astype(jnp.bfloat16)
        place_tok = jnp.sum(place_hot, axis=1)
        send_rows = jnp.einsum('tec,td->ecd', place_tok, h_norm, preferred_element_type=jnp.float32).astype(jnp.bfloat16)
        send_rows = send_rows.reshape(ep_size, local_experts, cap_slots, d_model)
        recv_rows = lax.all_to_all(send_rows, 'ep', 0, 2, tiled=True)
        recv_rows = recv_rows.reshape(local_experts, ep_size * cap_slots, d_model)
        gate_val = jnp.einsum('emd,edf->emf', recv_rows, ex_gate, preferred_element_type=jnp.float32)
        up_val = jnp.einsum('emd,edf->emf', recv_rows, ex_up, preferred_element_type=jnp.float32)
        act_val = (jax.nn.silu(gate_val) * up_val).astype(jnp.bfloat16)
        exp_out = jnp.einsum('emf,efd->emd', act_val, ex_down, preferred_element_type=jnp.float32).astype(jnp.bfloat16)
        exp_out = exp_out.reshape(1, local_experts, ep_size * cap_slots, d_model)
        back_rows = lax.all_to_all(exp_out, 'ep', 2, 0, tiled=True)
        back_rows = back_rows.reshape(num_experts, cap_slots, d_model)
        picked = jnp.einsum('tkec,ecd->tkd', place_hot, back_rows, preferred_element_type=jnp.float32)
        routed = jnp.sum(route_w[:, :, None] * picked, axis=1)
        out_hidden = (resid_bf.astype(jnp.float32) + shared_out + routed).astype(jnp.bfloat16)
        return out_hidden, lat_out, rope_out

    in_specs = (row_two, row_three, row_three, row_one, row_two, rep_one, rep_two, rep_two, rep_three, rep_three, rep_two, rep_one, rep_two, rep_two, rep_two, rep_two, exp_spec, exp_spec, exp_spec)
    out_specs = (row_two, row_three, row_three)
    return jax.shard_map(local_step, mesh=mesh, in_specs=in_specs, out_specs=out_specs, check_vma=False)
```

profile of v0, /device:TPU:112, one launch (start us, length us, event | category | flops | bytes accessed | tf_op | source)
XLA Modules:
  0.0 308.6 jit_solution(15284469383055055679)
XLA Ops:
  0.7 0.8 convert_element_type.96
  1.5 1.4 iota_compare_fusion.3
  2.8 1.3 convert_reduce_fusion
  4.1 0.7 iota_compare_fusion
  4.9 0.7 convert_element_type.89
  5.6 1.2 fusion.41
  6.8 1.9 fusion.52
  9.0 0.7 copy.48
  9.8 6.7 %convolution_convert_fusion.1 = bf16[128,3072]{1,0:T(8,128)(2,1)S(1)} fusion(bf16[2048,3072]{1,0:T(8,128)(2,1)} %param.25, bf16[128,2048]{1,0:T(8,128)(2,1)} %param.19, f32[2048]{0:T(1024)S(1)} %convert_element_type.89, f32[128]{0:T(128)S(1)} %add_rsqrt_fusion.2), kind=kOutput, calls=%fused_computation.15 | convolution fusion | flops 1612054528 | bytes 13902336 | tf_op jit(solution)/shard_map/dot_general | solution.py:36
  17.5 1.3 broadcast_select_fusion.1
  18.8 3.8 %copy.50 = bf16[128,64,64]{2,1,0:T(8,128)(2,1)} copy(bf16[128,64,64]{0,2,1:T(8,128)(2,1)S(1)} %broadcast_select_fusion.1) | data formatting | bytes 2097152 | tf_op jit(solution)/shard_map/jit(_where)/select_n | solution.py:47
  22.8 2.3 convert_bitcast_fusion.1
  25.1 5.0 %broadcast_select_fusion = bf16[128,64,512]{2,1,0:T(8,128)(2,1)S(1)} fusion(bf16[128,64,512]{2,1,0:T(8,128)(2,1)} %param.20, pred[128,64]{1,0:T(8,128)(4,1)} %get-tuple-element.14, bf16[128,512]{1,0:T(8,128)(2,1)S(1)} %copy.44), kind=kLoop, calls=%fused_computation.2 | loop fusion | flops 4194304 | bytes 16916480 | tf_op jit(solution)/shard_map/jit(_where)/select_n | solution.py:46
  30.7 1.2 fusion.45
  31.9 2.5 fusion.32
  34.4 0.7 fusion.60
  35.1 8.5 %convolution_convert_fusion.2 = bf16[128,16,512]{2,1,0:T(8,128)(2,1)} fusion(bf16[128,64,512]{2,1,0:T(8,128)(2,1)} %copy-done.2, f32[128,16]{1,0:T(8,128)S(1)} %fusion.60, f32[128,16,64]{2,1,0:T(8,128)S(1)} %fusion.32), kind=kOutput, calls=%fused_computation.31 | convolution fusion | flops 135661632 | bytes 11018240 | tf_op jit(solution)/shard_map/bhs,bsc->bhc/dot_general | solution.py:54
  43.5 4.9 %fusion.35 = bf16[16,128,128]{1,2,0:T(8,128)(2,1)S(1)} fusion(bf16[16,512,128]{2,1,0:T(8,128)(2,1)} %param.28, bf16[128,16,512]{2,1,0:T(8,128)(2,1)} %convolution_convert_fusion.2), kind=kOutput, calls=%fused_computation.39 | convolution fusion | flops 268697600 | bytes 4718592 | tf_op jit(solution)/shard_map/bhc,hcv->bhv/dot_general | solution.py:55
  48.5 4.8 %multiply_reduce_fusion = (f32[128]{0:T(128)S(1)}, f32[128,2048]{1,0:T(8,128)S(1)}) fusion(bf16[128,2048]{0,1:T(8,128)(2,1)S(1)} %bitcast.66, bf16[2048,2048]{1,0:T(8,128)(2,1)} %param.29, bf16[128,2048]{1,0:T(8,128)(2,1)S(1)} %copy-done.3), kind=kOutput, calls=%fused_computation.48 | convolution fusion | flops 1075314560 | bytes 10486272 | tf_op jit(solution)/shard_map/dot_general | solution.py:56
  53.7 0.5 fusion.13
  54.2 2.1 convolution_convert_fusion
  56.4 77.3 %all_to_all.30 = bf16[8,8,24,2048]{3,2,1,0:T(8,128)(2,1)S(1)} all-to-all(bf16[8,8,24,2048]{3,2,1,0:T(8,128)(2,1)S(1)} %bitcast.60), channel_id=1, replica_groups=mesh['dp'=2,'ep'=8] {'ep'}, dimensions={0} | all-to-all | bytes 12582912 | tf_op jit(solution)/shard_map/all_to_all | solution.py:106
  133.7 3.3 %copy.57 = bf16[1,8,8,24,2048]{4,3,2,1,0:T(8,128)(2,1)} copy(bf16[1,8,8,24,2048]{4,3,1,2,0:T(8,128)(2,1)S(1)} %bitcast.61) | data formatting | bytes 12582912 | tf_op jit(solution)/shard_map/all_to_all | solution.py:106
  137.0 22.2 %fusion.61 = f32[8,192,1408]{2,1,0:T(8,128)} fusion(bf16[8,192,2048]{2,1,0:T(8,128)(2,1)} %bitcast.62, bf16[8,2048,1408]{2,1,0:T(8,128)(2,1)} %param.35), kind=kOutput, calls=%fused_computation.88 | convolution fusion | flops 8858370048 | bytes 61079552 | tf_op jit(solution)/shard_map/emd,edf->emf/dot_general | solution.py:108
  159.2 24.9 %multiply_convert_fusion.clone.6 = bf16[8,192,1408]{2,1,0:T(8,128)(2,1)} fusion(f32[8,192,1408]{2,1,0:T(8,128)} %fusion.61, bf16[8,192,2048]{2,1,0:T(8,128)(2,1)} %bitcast.63, bf16[8,2048,1408]{2,1,0:T(8,128)(2,1)} %param.36), kind=kOutput, calls=%fused_computation.1.clone.clone.clone.clone.clone.1 | convolution fusion | flops 8871346176 | bytes 65404928 | tf_op jit(solution)/shard_map/emd,edf->emf/dot_general | solution.py:109
  184.1 18.9 %convert_bitcast_fusion = bf16[1,8,192,2048]{3,2,1,0:T(8,128)(2,1)S(1)} fusion(bf16[8,1408,2048]{2,1,0:T(8,128)(2,1)} %param.37, bf16[8,192,1408]{2,1,0:T(8,128)(2,1)} %multiply_convert_fusion.clone.6), kind=kOutput, calls=%fused_computation.8 | convolution fusion | flops 8861515776 | bytes 56754176 | tf_op jit(solution)/shard_map/emf,efd->emd/dot_general | solution.py:111
  203.1 6.1 %copy.58 = bf16[1,8,192,2048]{3,1,0,2:T(8,128)(2,1)} copy(bf16[1,8,192,2048]{3,2,1,0:T(8,128)(2,1)S(1)} %convert_bitcast_fusion) | data formatting | bytes 12582912 | tf_op jit(solution)/shard_map/reshape | solution.py:112
  209.2 5.1 %all-to-all-start.1 = ((bf16[1,8,192,2048]{3,1,0,2:T(8,128)(2,1)}), bf16[1,8,192,2048]{3,1,0,2:T(8,128)(2,1)}, u32[]{:S(2)}, u32[]{:S(2)}) async-start(bf16[1,8,192,2048]{3,1,0,2:T(8,128)(2,1)} %copy.58), calls=%async_computation.1 | async-start | bytes 12582912 | tf_op jit(solution)/shard_map/all_to_all | solution.py:113
  214.7 7.2 %fusion.59 = f32[128,2816]{1,0:T(8,128)} fusion(bf16[2048,2816]{1,0:T(8,128)(2,1)} %param.32, f32[128,2048]{1,0:T(8,128)S(1)} %get-tuple-element.16, f32[2048]{0:T(1024)S(1)} %convert_element_type.104, f32[128]{0:T(128)S(1)} %add_rsqrt_fusion), kind=kOutput, calls=%fused_computation.86 | convolution fusion | flops 1477181440 | bytes 14033408 | tf_op jit(solution)/shard_map/dot_general | solution.py:72
  221.9 64.2 %all-to-all-done.1 = bf16[1,8,192,2048]{3,1,0,2:T(8,128)(2,1)} async-done(((bf16[1,8,192,2048]{3,1,0,2:T(8,128)(2,1)}), bf16[1,8,192,2048]{3,1,0,2:T(8,128)(2,1)}, u32[]{:S(2)}, u32[]{:S(2)}) %all-to-all-start.1) | async-done | bytes 6291488 | tf_op jit(solution)/shard_map/all_to_all | solution.py:113
  286.1 9.3 %fusion.3 = f32[128,2048]{1,0:T(8,128)} fusion(f32[128,6]{0,1:T(8,128)S(1)} %multiply_divide_fusion, bf16[1,8,8,24,2048]{4,1,3,2,0:T(8,128)(2,1)} %bitcast.10, pred[128,6,24]{0,2,1:T(8,128)(4,1)S(1)} %iota_compare_fusion.1, pred[128,6,64]{0,2,1:T(8,128)(4,1)S(1)} %iota_compare_fusion), kind=kOutput, calls=%fused_computation.6 | convolution fusion | flops 4835901440 | bytes 7410688 | tf_op jit(solution)/shard_map/tkec,ecd->tkd/dot_general | solution.py:115
  295.4 12.7 %fusion.12 = bf16[128,2048]{1,0:T(8,128)(2,1)} fusion(f32[128,2048]{1,0:T(8,128)} %fusion.3, f32[128,2048]{1,0:T(8,128)S(1)} %get-tuple-element.16, bf16[2816,2048]{1,0:T(8,128)(2,1)} %param.34, bf16[2048,2816]{1,0:T(8,128)(2,1)} %param.33, f32[128,2816]{1,0:T(8,128)} %fusion.59, f32[2048]{0:T(1024)S(1)} %convert_element_type.104, f32[128]{0:T(128)S(1)} %add_rsqrt_fusion), kind=kOutput, calls=%fused_computation.22 | convolution fusion | flops 2956525568 | bytes 27140608 | tf_op jit(solution)/shard_map/dot_general | solution.py:75
  (52 shorter events, 2.9 us)
Async XLA Ops:
  0.6 6.2 %copy-start = (bf16[2048,576]{0,1:T(8,128)(2,1)S(1)}, bf16[2048,576]{0,1:T(8,128)(2,1)}, u32[]{:S(2)}) copy-start(bf16[2048,576]{0,1:T(8,128)(2,1)} %param.26) | copy-start | bytes 7077892
  9.8 7.6 %copy-start.8 = (pred[128,64]{1,0:T(8,128)(4,1)S(1)}, pred[128,64]{1,0:T(8,128)(4,1)}, u32[]{:S(2)}) copy-start(pred[128,64]{1,0:T(8,128)(4,1)} %get-tuple-element.14) | copy-start | bytes 24580
  18.8 11.3 %copy-start.5 = (bf16[128,64,64]{0,2,1:T(8,128)(2,1)}, bf16[128,64,64]{0,2,1:T(8,128)(2,1)S(1)}, u32[]{:S(2)}) copy-start(bf16[128,64,64]{0,2,1:T(8,128)(2,1)S(1)} %broadcast_select_fusion.1) | copy-start | bytes 3145732
  25.1 5.1 %copy-start.7 = (f32[128,32]{1,0:T(8,128)S(1)}, f32[128,32]{1,0:T(8,128)}, u32[]{:S(2)}) copy-start(f32[128,32]{1,0:T(8,128)} %copy.48) | copy-start | bytes 49156
  25.1 5.6 %copy-start.4 = (bf16[128,64,64]{2,1,0:T(8,128)(2,1)S(1)}, bf16[128,64,64]{2,1,0:T(8,128)(2,1)}, u32[]{:S(2)}) copy-start(bf16[128,64,64]{2,1,0:T(8,128)(2,1)} %copy.50) | copy-start | bytes 3145732
  30.2 4.2 %copy-start.2 = (bf16[128,64,512]{2,1,0:T(8,128)(2,1)}, bf16[128,64,512]{2,1,0:T(8,128)(2,1)S(1)}, u32[]{:S(2)}) copy-start(bf16[128,64,512]{2,1,0:T(8,128)(2,1)S(1)} %broadcast_select_fusion) | copy-start | bytes 25165828
  30.2 1.7 copy-start.10
  35.1 13.4 %copy-start.3 = (bf16[128,2048]{1,0:T(8,128)(2,1)S(1)}, bf16[128,2048]{1,0:T(8,128)(2,1)}, u32[]{:S(2)}) copy-start(bf16[128,2048]{1,0:T(8,128)(2,1)} %param.19) | copy-start | bytes 1572868
  48.5 4.8 %copy-start.9 = (s32[128,64]{0,1:T(8,128)S(1)}, s32[128,64]{0,1:T(8,128)}, u32[]{:S(2)}) copy-start(s32[128,64]{0,1:T(8,128)} %convert_reduce_fusion) | copy-start | bytes 98308
  48.5 5.2 %copy-start.11 = (s32[128,6]{0,1:T(8,128)S(1)}, s32[128,6]{0,1:T(8,128)}, u32[]{:S(2)}) copy-start(s32[128,6]{0,1:T(8,128)} %param.23) | copy-start | bytes 9220
  48.5 5.2 %copy-start.12 = (bf16[2048]{0:T(1024)(128)(2,1)S(1)}, bf16[2048]{0:T(1024)(128)(2,1)}, u32[]{:S(2)}) copy-start(bf16[2048]{0:T(1024)(128)(2,1)} %param.30) | copy-start | bytes 12292
  209.2 5.1 %copy-start.6 = (bf16[2048,64]{0,1:T(8,128)(2,1)S(1)}, bf16[2048,64]{0,1:T(8,128)(2,1)}, u32[]{:S(2)}) copy-start(bf16[2048,64]{0,1:T(8,128)(2,1)} %param.31) | copy-start | bytes 786436
  209.2 77.0 %all-to-all-start.1 = ((bf16[1,8,192,2048]{3,1,0,2:T(8,128)(2,1)}), bf16[1,8,192,2048]{3,1,0,2:T(8,128)(2,1)}, u32[]{:S(2)}, u32[]{:S(2)}) async-start(bf16[1,8,192,2048]{3,1,0,2:T(8,128)(2,1)} %copy.58), calls=%async_computation.1 | async-start | bytes 12582912 | tf_op jit(solution)/shard_map/all_to_all | solution.py:113
  295.4 12.7 %copy-start.1 = (bf16[2048,576]{0,1:T(8,128)(2,1)S(1)}, bf16[2048,576]{0,1:T(8,128)(2,1)}, u32[]{:S(2)}) copy-start(bf16[2048,576]{0,1:T(8,128)(2,1)} %param.26) | copy-start | bytes 7077892
where the time goes:
time: 314 us; the launch traced here: 309 us
  matrix products  131 us (42%)
  blocking collectives  77.3 us (25%)
  waiting for transfers between devices  64.2 us (20%)
  local copies, waits for them, and re-layouts  15.2 us (5%)
  other arithmetic  14.7 us (5%)
  starting transfers between devices  5.05 us (2%)
    all_to_all x1, blocking collectives, local_step(): recv_rows = lax.all_to_all(send_rows, 'ep', 0, 2, tiled=True)  77.3 us
    all_to_all x1, waiting for transfers between devices, local_step(): back_rows = lax.all_to_all(exp_out, 'ep', 2, 0, tiled=True)  64.2 us
    dot_general x1, matrix products, local_step(): jnp.einsum('emd,edf->emf', recv_rows, ex_up, preferred_element_type=jnp.f...  24.9 us
    dot_general x1, matrix products, local_step(): jnp.einsum('emd,edf->emf', recv_rows, ex_gate, preferred_element_type=jnp...  22.2 us
    dot_general x1, matrix products, local_step(): jnp.einsum('emf,efd->emd', act_val, ex_down, preferred_element_type=jnp.f...  18.9 us
    dot_general x1, matrix products, swiglu_shared(): return jnp.dot(act_val, sh_down, preferred_element_type=jnp.float32)  12.7 us
    dot_general x1, matrix products, local_step(): jnp.einsum('tkec,ecd->tkd', place_hot, back_rows, preferred_element_type=...  9.31 us
    dot_general x1, matrix products, attention_block(): jnp.einsum('bhs,bsc->bhc', prob_mat, lat_out, preferred_element_type=jnp....  8.47 us
  transfers between devices with their start and end apart: 1, of which 1 were waited for; matrix products, arithmetic and copies ran while one was open for 2% of the time, Pallas kernels for 0%

commit v1 on v0

v1 whole, which is shorter than its diff:
```python
import functools

import jax
import jax.numpy as jnp
from jax import lax
from jax.experimental import pallas as pl
from jax.experimental.pallas import tpu as pltpu
from jax.sharding import PartitionSpec as P

ROUTE_SCALE = 2.827
ROPE_BASE = 10000.0
NORM_EPS = 1e-6
F32 = jnp.float32
BF16 = jnp.bfloat16
VMEM_LIMIT = 67_043_328

GROUP = 8
CHUNK = 256


def unit_norm(values):
    mean_sq = jnp.mean(jnp.square(values), axis=-1, keepdims=True)
    return values * lax.rsqrt(mean_sq + NORM_EPS)


def mm(a, b):
    return jnp.dot(a, b, preferred_element_type=F32)


def mm_nt(a, b):
    return lax.dot_general(a, b, (((1,), (1,)), ((), ())), preferred_element_type=F32)


def attention_kernel(
    pos_smem, x_ref, pos_ref, freq_ref, gain_a_ref, gain_f_ref, lat_ref, rope_ref,
    wq_hbm, wkv_hbm, wuk_hbm, wuv_hbm, wo_hbm,
    lat_out, rope_out, resid_ref, h_ref,
    wq, wkv, wuk_even, wuk_odd, wuv, wo, qc, qr, olat, c_scr, k_scr, heads_scr, sem,
):
    step = pl.program_id(0)
    heads, nope, rank = wuk_hbm.shape
    rope_dim = rope_ref.shape[-1]
    rows, d_model = x_ref.shape
    seq = lat_ref.shape[1]
    pairs = heads // 2
    pair_cols = 2 * (nope + rope_dim)
    per_copy = 2
    copies = pairs // per_copy
    wide = per_copy * pair_cols

    def q_copy(i):
        cols = pl.ds(i * wide, wide)
        return pltpu.make_async_copy(wq_hbm.at[:, cols], wq.at[:, cols], sem.at[i])

    kv_copy = pltpu.make_async_copy(wkv_hbm, wkv, sem.at[copies])
    uv_copy = pltpu.make_async_copy(wuv_hbm, wuv, sem.at[copies + 1])
    wo_copy = pltpu.make_async_copy(wo_hbm, wo, sem.at[copies + 2])

    def uk_copies(i):
        even = pltpu.make_async_copy(wuk_hbm.at[2 * i], wuk_even.at[i], sem.at[copies + 3 + 2 * i])
        odd = pltpu.make_async_copy(wuk_hbm.at[2 * i + 1], wuk_odd.at[i, rope_dim : rope_dim + nope], sem.at[copies + 4 + 2 * i])
        return even, odd

    @pl.when(step == 0)
    def _():
        kv_copy.start()
        for i in range(copies):
            q_copy(i).start()
            for j in range(per_copy):
                for c in uk_copies(i * per_copy + j):
                    c.start()
        uv_copy.start()
        wo_copy.start()
        zero = jnp.zeros((pairs, rope_dim, rank), BF16)
        wuk_odd[:, :rope_dim] = zero
        wuk_odd[:, rope_dim + nope :] = zero
        x_norm = (unit_norm(x_ref[...].astype(F32)) * gain_a_ref[...].astype(F32)).astype(BF16)
        angle = pos_ref[...].astype(F32) * freq_ref[...]
        cos, sin = jnp.cos(angle), jnp.sin(angle)
        lane = lax.broadcasted_iota(jnp.int32, (rows, 2 * rope_dim), 1)
        first = lax.rem(lane, rope_dim) < rope_dim // 2

        def rope(v):
            ahead = pltpu.roll(v, 2 * rope_dim - rope_dim // 2, 1)
            behind = pltpu.roll(v, rope_dim // 2, 1)
            return (v * cos + jnp.where(first, -ahead, behind) * sin).astype(BF16)

        kv_copy.wait()
        kv = mm(x_norm, wkv[...])
        c_scr[...] = unit_norm(kv[:, :rank]).astype(BF16).astype(F32)
        k_part = kv[:, rank:]
        k_scr[...] = rope(jnp.concatenate([k_part, k_part], axis=1)).astype(F32)
        for i in range(pairs):
            if i % per_copy == 0:
                q_copy(i // per_copy).wait()
            for c in uk_copies(i):
                c.wait()
            q = mm(x_norm, wq[:, i * pair_cols : (i + 1) * pair_cols]).astype(BF16)
            qc[2 * i] = mm(q[:, :nope], wuk_even[i]).astype(BF16).astype(F32)
            qc[2 * i + 1] = mm(q[:, nope:], wuk_odd[i]).astype(BF16).astype(F32)
            both = jnp.where(lane < rope_dim, q[:, nope : 2 * nope].astype(F32), q[:, 2 * nope :].astype(F32))
            turned = rope(both).astype(F32)
            qr[2 * i] = turned
            qr[2 * i + 1] = pltpu.roll(turned, rope_dim, 1)

    at = pl.ds(pl.multiple_of(step * GROUP, GROUP), GROUP)
    c_new = c_scr[at, :]
    k_new = k_scr[at, :rope_dim]
    slot_lat = lax.broadcasted_iota(jnp.int32, (seq, rank), 0)
    slot_rope = lax.broadcasted_iota(jnp.int32, (seq, rope_dim), 0)
    for t in range(GROUP):
        pos = pos_smem[step * GROUP + t]
        lat_out[t] = jnp.where(slot_lat == pos, c_new[t : t + 1, :], lat_ref[t].astype(F32)).astype(BF16)
        rope_out[t] = jnp.where(slot_rope == pos, k_new[t : t + 1, :], rope_ref[t].astype(F32)).astype(BF16)
    keys = lat_out[...].reshape(GROUP * seq, rank)
    keys_rope = rope_out[...].reshape(GROUP * seq, rope_dim)
    q_lat = qc[:, at, :].reshape(heads * GROUP, rank).astype(BF16)
    q_rope = qr[:, at, :].reshape(heads * GROUP, 2 * rope_dim).astype(BF16)[:, :rope_dim]
    scores = (mm_nt(q_lat, keys) + mm_nt(q_rope, keys_rope)) * (nope + rope_dim) ** -0.5
    key_id = lax.broadcasted_iota(jnp.int32, (GROUP, GROUP * seq), 1)
    low = lax.broadcasted_iota(jnp.int32, (GROUP, GROUP * seq), 0) * seq
    seen = (key_id >= low) & (key_id <= low + pos_ref[at, :])
    scores = jnp.where(seen[None], scores.reshape(heads, GROUP, GROUP * seq), -jnp.inf)
    expd = jnp.exp(scores - jnp.max(scores, axis=-1, keepdims=True))
    prob = (expd / jnp.sum(expd, axis=-1, keepdims=True)).astype(BF16)
    out = mm(prob.reshape(heads * GROUP, GROUP * seq), keys).astype(BF16).astype(F32)
    olat[:, at, :] = out.reshape(heads, GROUP, rank)

    @pl.when(step == pl.num_programs(0) - 1)
    def _():
        uv_copy.wait()
        v_dim = wuv.shape[-1]
        for h in range(heads):
            heads_scr[:, h * v_dim : (h + 1) * v_dim] = mm(olat[h].astype(BF16), wuv[h]).astype(BF16)
        wo_copy.wait()
        piece = 512
        for n in range(0, d_model, piece):
            part = mm(heads_scr[...], wo[:, n : n + piece])
            resid_ref[:, n : n + piece] = (x_ref[:, n : n + piece].astype(F32) + part).astype(BF16)
        h_ref[...] = (unit_norm(resid_ref[...].astype(F32)) * gain_f_ref[...].astype(F32)).astype(BF16)


def attention(tok_in, lat_cache, rope_cache, tok_pos, attn_gain, w_query, w_kvdown, w_ukey, w_uval, w_out, ffn_gain):
    rows, d_model = tok_in.shape
    _, seq, rank = lat_cache.shape
    rope_dim = rope_cache.shape[-1]
    heads, nope, _ = w_ukey.shape
    v_dim = w_uval.shape[-1]
    inv_freq = ROPE_BASE ** (-(2.0 * jnp.arange(rope_dim // 2)) / rope_dim)
    freq = jnp.tile(inv_freq, 4)[None, :]

    def const(shape):
        return pl.BlockSpec(shape, lambda g, *_: (0,) * len(shape))

    any_spec = pl.BlockSpec(memory_space=pl.ANY)
    lat_spec = pl.BlockSpec((GROUP, seq, rank), lambda g, *_: (g, 0, 0))
    rope_spec = pl.BlockSpec((GROUP, seq, rope_dim), lambda g, *_: (g, 0, 0))
    grid_spec = pltpu.PrefetchScalarGridSpec(
        num_scalar_prefetch=1,
        grid=(rows // GROUP,),
        in_specs=[const((rows, d_model)), const((rows, 1)), const((1, 2 * rope_dim)), const((1, d_model)), const((1, d_model)),
                  lat_spec, rope_spec] + [any_spec] * 5,
        out_specs=[lat_spec, rope_spec, const((rows, d_model)), const((rows, d_model))],
        scratch_shapes=[
            pltpu.VMEM(w_query.shape, BF16),
            pltpu.VMEM(w_kvdown.shape, BF16),
            pltpu.VMEM((heads // 2, nope, rank), BF16),
            pltpu.VMEM((heads // 2, nope + 2 * rope_dim, rank), BF16),
            pltpu.VMEM(w_uval.shape, BF16),
            pltpu.VMEM(w_out.shape, BF16),
            pltpu.VMEM((heads, rows, rank), F32),
            pltpu.VMEM((heads, rows, 2 * rope_dim), F32),
            pltpu.VMEM((heads, rows, rank), F32),
            pltpu.VMEM((rows, rank), F32),
            pltpu.VMEM((rows, 2 * rope_dim), F32),
            pltpu.VMEM((rows, heads * v_dim), BF16),
            pltpu.SemaphoreType.DMA((heads // 4 + 3 + heads,)),
        ],
    )
    return pl.pallas_call(
        attention_kernel,
        name="attention",
        grid_spec=grid_spec,
        out_shape=[
            jax.ShapeDtypeStruct(lat_cache.shape, BF16),
            jax.ShapeDtypeStruct(rope_cache.shape, BF16),
            jax.ShapeDtypeStruct((rows, d_model), BF16),
            jax.ShapeDtypeStruct((rows, d_model), BF16),
        ],
        compiler_params=pltpu.CompilerParams(vmem_limit_bytes=VMEM_LIMIT, dimension_semantics=("arbitrary",)),
    )(tok_pos, tok_in, tok_pos[:, None], freq, attn_gain[None, :], ffn_gain[None, :], lat_cache, rope_cache,
      w_query, w_kvdown, w_ukey, w_uval, w_out)


def moe_kernel(
    ep, slots, h_in, resid_ref, ids_ref, wr_ref,
    shg, shu, shd, exg, exu, exd,
    out_ref,
    wbuf, h_all, w_send, w_all, pick, weigh, comb, x_all, acts, acts_sh, e_buf,
    part, part_peer, from_peer, transit, final, sh_acc,
    w_sem, b_sem, ag_send, ag_recv, rt_send, rt_recv, rs_send, rs_recv,
):
    rows, d_model = h_in.shape
    local, _, ff = exg.shape
    chips = ep // 2
    half = rows // 2
    pair_slots = 2 * slots
    shared_parts = shg.shape[1] // ff
    chunks = d_model // CHUNK
    per_slot = ff // CHUNK
    me = lax.axis_index("ep")
    chip, core = me // 2, lax.rem(me, 2)

    def device(chip_step, other_core):
        side = 1 - core if other_core else core
        return lax.rem(chip + chip_step, chips) * 2 + side

    right, left, peer = device(1, False), device(chips - 1, False), device(0, True)

    def remote(src, dst, send, recv, to):
        return pltpu.make_async_remote_copy(
            src_ref=src, dst_ref=dst, send_sem=send, recv_sem=recv,
            device_id={"ep": to}, device_id_type=pl.DeviceIdType.MESH)

    def shared_copies(i):
        cols = pl.ds(i * ff, ff)
        return [pltpu.make_async_copy(src.at[:, cols], wbuf.at[i % 2, k], w_sem.at[i % 2, k]) for k, src in enumerate((shg, shu))]

    def expert_copies(e):
        s = lax.rem(e, 2)
        return [pltpu.make_async_copy(src.at[e], wbuf.at[s, k], w_sem.at[s, k]) for k, src in enumerate((exg, exu))]

    def down_copy(c, k):
        s = lax.rem(c, 2)
        cols = pl.ds(pl.multiple_of(c * CHUNK, CHUNK), CHUNK)
        src = exd.at[k, :, cols] if k < local else shd.at[pl.ds((k - local) * ff, ff), cols]
        return pltpu.make_async_copy(src, down_tile(c, k), b_sem.at[s, k])

    def down_tile(c, k):
        return wbuf.at[lax.rem(c, 2), k // per_slot, pl.ds(0, ff), pl.ds((k % per_slot) * CHUNK, CHUNK)]

    def start_down(c):
        for k in range(local + shared_parts):
            down_copy(c, k).start()

    for i in range(shared_parts):
        for c in shared_copies(i):
            c.start()

    barrier = pltpu.get_barrier_semaphore()
    others = [(dc, oc) for dc in range(chips) for oc in (False, True) if dc or oc]
    for dc, oc in others:
        pl.semaphore_signal(barrier, inc=1, device_id={"ep": device(dc, oc)}, device_id_type=pl.DeviceIdType.MESH)
    pl.semaphore_wait(barrier, len(others))

    top, low = pl.ds(0, half), pl.ds(half, half)
    top_o, low_o = pl.ds(rows, half), pl.ds(rows + half, half)
    back, far = chips - 1, chips - 2

    def gather_copy(i):
        src, dst, to = (
            (h_in, h_all.at[0, pl.ds(rows, rows)], peer),
            (h_in.at[top], h_all.at[back, top], right),
            (h_in.at[low], h_all.at[back, low], right),
            (h_in.at[low], h_all.at[1, low], left),
            (h_in.at[top], h_all.at[1, top], left),
            (h_all.at[back, top], h_all.at[far, top], right),
            (h_all.at[1, low], h_all.at[far, low], left),
            (h_all.at[back, top], h_all.at[back, top_o], peer),
            (h_all.at[1, low], h_all.at[1, low_o], peer),
            (h_all.at[back, low], h_all.at[back, low_o], peer),
            (h_all.at[1, top], h_all.at[1, top_o], peer),
            (h_all.at[far, top], h_all.at[far, top_o], peer),
            (h_all.at[far, low], h_all.at[far, low_o], peer),
        )[i]
        return remote(src, dst, ag_send.at[i], ag_recv.at[i], to)

    for i in range(5):
        gather_copy(i).start()

    logits = mm_nt(wr_ref[...], h_in[...])
    gate = jax.nn.sigmoid(logits)
    expert_id = lax.broadcasted_iota(jnp.int32, logits.shape, 0)
    listed = expert_id == ids_ref[0:1, :]
    for k in range(1, ids_ref.shape[0]):
        listed = listed | (expert_id == ids_ref[k : k + 1, :])
    total = jnp.sum(jnp.where(listed, gate, 0.0), axis=0, keepdims=True)
    w_send[...] = jnp.where(listed, ROUTE_SCALE * gate / total, -1.0)

    def mine(d):
        return pl.ds(pl.multiple_of(d * local, local), local)

    def route_copy(i):
        dc, oc = others[i]
        d = device(dc, oc)
        return remote(w_send.at[mine(d)], w_all.at[(chips - dc) % chips, int(oc)], rt_send.at[i], rt_recv.at[i], d)

    for i in range(len(others)):
        route_copy(i).start()
    w_all[0, 0] = w_send[mine(me), :]
    h_all[0, :rows] = h_in[...]

    def up(x, s, act):
        for n in range(0, ff, 512):
            cols = pl.ds(n, min(512, ff - n))
            g = mm(x[...], wbuf[s, 0, :, cols])
            u = mm(x[...], wbuf[s, 1, :, cols])
            act[:, cols] = (jax.nn.silu(g) * u).astype(BF16)

    earlier = lax.broadcasted_iota(jnp.int32, (rows, rows), 0) < lax.broadcasted_iota(jnp.int32, (rows, rows), 1)
    tri = jnp.where(earlier, 1.0, 0.0).astype(BF16)
    slot_id = lax.broadcasted_iota(jnp.int32, (pair_slots, 2 * rows), 0).astype(F32)

    def place(r):
        ranks, weights = [], []
        for q in range(2):
            w = w_all[r, q]
            has = w >= 0.0
            rank = mm(jnp.where(has, 1.0, 0.0).astype(BF16), tri)
            ranks.append(jnp.where(has, rank + q * slots, -1.0))
            weights.append(w)
        rank, w = jnp.concatenate(ranks, axis=1), jnp.concatenate(weights, axis=1)
        for e in range(local):
            at = pl.ds(e * pair_slots, pair_slots)
            hit = slot_id == rank[e : e + 1, :]
            pick[at, :] = jnp.where(hit, 1.0, 0.0).astype(BF16)
            weigh[at, :] = jnp.where(hit, w[e : e + 1, :], 0.0)
        rest = weigh[...].T
        for k in range(3):
            piece = rest.astype(BF16)
            comb[r, pl.ds(k * 2 * rows, 2 * rows), :] = piece
            rest = rest - piece.astype(F32)

        @pl.loop(0, d_model // 512)
        def _(n):
            cols = pl.ds(pl.multiple_of(n * 512, 512), 512)
            x = mm(pick[...], h_all[r, :, cols]).astype(BF16)
            for e in range(local):
                x_all[e, pl.ds(r * pair_slots, pair_slots), cols] = x[e * pair_slots : (e + 1) * pair_slots]

    def wait_recv(*ids):
        for i in ids:
            gather_copy(i).wait_recv()

    for c in shared_copies(0):
        c.wait()
    up(h_in, 0, acts_sh.at[0])
    for c in expert_copies(0):
        c.start()
    wait_recv(1, 3)
    for i in (5, 6, 7, 8):
        gather_copy(i).start()
    for c in shared_copies(1):
        c.wait()
    up(h_in, 1, acts_sh.at[1])
    for c in expert_copies(1):
        c.start()
    for i in range(len(others)):
        route_copy(i).wait_recv()
    wait_recv(0)
    place(0)
    wait_recv(2, 4)
    for i in (9, 10):
        gather_copy(i).start()
    wait_recv(7, 9)
    place(back)
    wait_recv(8, 10)
    place(1)
    wait_recv(5, 6)
    for i in (11, 12):
        gather_copy(i).start()
    wait_recv(11, 12)
    place(far)

    @pl.loop(0, local)
    def _(e):
        for c in expert_copies(e):
            c.wait()
        up(x_all.at[e], lax.rem(e, 2), acts.at[e])

        @pl.when(e < local - 2)
        def _():
            for c in expert_copies(e + 2):
                c.start()

        @pl.when(e >= local - 2)
        def _():
            start_down(e - (local - 2))

    def rs_copy(i, c):
        src, dst, to = (
            (part_peer.at[c], from_peer.at[c], peer),
            (part.at[c, far, top], transit.at[0, c], right),
            (part.at[c, far, low], transit.at[1, c], left),
            (part.at[c, 1, low], final.at[0, c, low], right),
            (part.at[c, back, top], final.at[1, c, top], left),
            (part.at[c, 1, top], final.at[0, c, top], right),
            (part.at[c, back, low], final.at[1, c, low], left),
        )[i]
        return remote(src, dst, rs_send.at[i, c], rs_recv.at[i, c], to)

    def add_peer(c):
        rs_copy(0, c).wait_recv()
        for r in (far, 1, back):
            part[c, r] += from_peer[c, r]
            if r == far:
                rs_copy(1, c).start()
                rs_copy(2, c).start()
        rs_copy(3, c).start()
        rs_copy(4, c).start()
        part[c, 0] += from_peer[c, 0]

    def pass_on(c):
        rs_copy(1, c).wait_recv()
        part[c, 1, top] += transit[0, c]
        rs_copy(5, c).start()
        rs_copy(2, c).wait_recv()
        part[c, back, low] += transit[1, c]
        rs_copy(6, c).start()

    @pl.loop(0, chunks)
    def _(c):
        for k in range(local):
            down_copy(c, k).wait()
            y = mm(acts[k], down_tile(c, k)[...]).astype(BF16)
            for r in range(chips):
                e_buf[r, k * pair_slots : (k + 1) * pair_slots, :] = y[r * pair_slots : (r + 1) * pair_slots]

        @pl.when(c >= 1)
        def _():
            add_peer(c - 1)

        for r in range(chips):
            z = mm(comb[r], e_buf[r])
            z = z[: 2 * rows] + z[2 * rows : 4 * rows] + z[4 * rows :]
            part[c, r] = z[:rows]
            part_peer[c, r] = z[rows:]
        rs_copy(0, c).start()

        shared = None
        for k in range(local, local + shared_parts):
            down_copy(c, k).wait()
            y = mm(acts_sh[k - local], down_tile(c, k)[...])
            shared = y if shared is None else shared + y
        sh_acc[c] = shared

        @pl.when(c + 2 < chunks)
        def _():
            start_down(c + 2)

        @pl.when(c >= 2)
        def _():
            pass_on(c - 2)

    add_peer(chunks - 1)
    pass_on(chunks - 2)
    pass_on(chunks - 1)
    for c in range(chunks):
        for i in (3, 4, 5, 6):
            rs_copy(i, c).wait_recv()
        cols = pl.ds(c * CHUNK, CHUNK)
        routed = part[c, 0] + final[0, c] + final[1, c]
        out_ref[:, cols] = (resid_ref[:, cols].astype(F32) + sh_acc[c] + routed).astype(BF16)
    for i in range(13):
        gather_copy(i).wait_send()
    for i in range(len(others)):
        route_copy(i).wait_send()

    @pl.loop(0, chunks)
    def _(c):
        for i in range(7):
            rs_copy(i, c).wait_send()


def moe(ep, h_norm, resid, expert_ids, w_router, sh_gate, sh_up, sh_down, ex_gate, ex_up, ex_down):
    rows, d_model = h_norm.shape
    top_k = expert_ids.shape[1]
    num_experts = w_router.shape[1]
    local, _, ff = ex_gate.shape
    chips = ep // 2
    slots = max(2, -(-2 * rows * top_k // num_experts))
    shared_parts = sh_gate.shape[1] // ff
    chunks = d_model // CHUNK
    pair_slots = 2 * slots
    dma = pltpu.SemaphoreType.DMA
    vmem = pl.BlockSpec(memory_space=pltpu.VMEM)
    any_spec = pl.BlockSpec(memory_space=pl.ANY)
    return pl.pallas_call(
        functools.partial(moe_kernel, ep, slots),
        name="experts",
        in_specs=[vmem] * 4 + [any_spec] * 6,
        out_specs=vmem,
        out_shape=jax.ShapeDtypeStruct((rows, d_model), BF16),
        scratch_shapes=[
            pltpu.VMEM((2, 2, d_model, ff), BF16),
            pltpu.VMEM((chips, 2 * rows, d_model), BF16),
            pltpu.VMEM((num_experts, rows), F32),
            pltpu.VMEM((chips, 2, local, rows), F32),
            pltpu.VMEM((local * pair_slots, 2 * rows), BF16),
            pltpu.VMEM((local * pair_slots, 2 * rows), F32),
            pltpu.VMEM((chips, 6 * rows, local * pair_slots), BF16),
            pltpu.VMEM((local, chips * pair_slots, d_model), BF16),
            pltpu.VMEM((local, chips * pair_slots, ff), BF16),
            pltpu.VMEM((shared_parts, rows, ff), BF16),
            pltpu.VMEM((chips, local * pair_slots, CHUNK), BF16),
            pltpu.VMEM((chunks, chips, rows, CHUNK), F32),
            pltpu.VMEM((chunks, chips, rows, CHUNK), F32),
            pltpu.VMEM((chunks, chips, rows, CHUNK), F32),
            pltpu.VMEM((2, chunks, rows // 2, CHUNK), F32),
            pltpu.VMEM((2, chunks, rows, CHUNK), F32),
            pltpu.VMEM((chunks, rows, CHUNK), F32),
            dma((2, 2)), dma((2, local + shared_parts)),
            dma((13,)), dma((13,)), dma((ep - 1,)), dma((ep - 1,)), dma((7, chunks)), dma((7, chunks)),
        ],
        compiler_params=pltpu.CompilerParams(vmem_limit_bytes=VMEM_LIMIT, collective_id=0, has_side_effects=True),
    )(h_norm, resid, expert_ids.T, w_router.T, sh_gate, sh_up, sh_down, ex_gate, ex_up, ex_down)


def solution(mesh):
    ep = mesh.shape["ep"]
    row_one = P(("dp", "ep"))
    row_two = P(("dp", "ep"), None)
    row_three = P(("dp", "ep"), None, None)
    rep_one = P(None)
    rep_two = P(None, None)
    rep_three = P(None, None, None)
    exp_spec = P("ep", None, None)

    def local_step(tok_in, lat_cache, rope_cache, tok_pos, expert_ids, attn_gain, w_query, w_kvdown, w_ukey, w_uval, w_out, ffn_gain, w_router, sh_gate, sh_up, sh_down, ex_gate, ex_up, ex_down):
        lat_out, rope_out, resid, h_norm = attention(tok_in, lat_cache, rope_cache, tok_pos, attn_gain, w_query, w_kvdown, w_ukey, w_uval, w_out, ffn_gain)
        out_hidden = moe(ep, h_norm, resid, expert_ids, w_router, sh_gate, sh_up, sh_down, ex_gate, ex_up, ex_down)
        return out_hidden, lat_out, rope_out

    in_specs = (row_two, row_three, row_three, row_one, row_two, rep_one, rep_two, rep_two, rep_three, rep_three, rep_two, rep_one, rep_two, rep_two, rep_two, rep_two, exp_spec, exp_spec, exp_spec)
    out_specs = (row_two, row_three, row_three)
    return jax.shard_map(local_step, mesh=mesh, in_specs=in_specs, out_specs=out_specs, check_vma=False)
```

time: 314 us -> 164 us (0.52); the launches traced: 309 us -> 163 us
  Pallas kernels: 0 us -> 143 us
  matrix products: 131 us -> 0 us
  blocking collectives: 77.3 us -> 0 us
  waiting for transfers between devices: 64.2 us -> 0 us
  other arithmetic: 14.7 us -> 0.01 us
  starting transfers between devices: 5.05 us -> 0 us
  local copies, waits for them, and re-layouts: 15.2 us -> 19.6 us
    pallas_call x0 -> x2, Pallas kernels: none -> 143 us  [the longest x1 113 us: moe(): pl.pallas_call(functools.partial(moe_kernel, ep, slots), name='experts',...]
    dot_general x16 -> x0, matrix products: 131 us -> none  [the longest x1 24.9 us: local_step(): jnp.einsum('emd,edf->emf', recv_rows, ex_up, preferred_element_type=jnp.f...]
    all_to_all x1 -> x0, blocking collectives: 77.3 us -> none  [local_step(): recv_rows = lax.all_to_all(send_rows, 'ep', 0, 2, tiled=True)]
    all_to_all x1 -> x0, waiting for transfers between devices: 64.2 us -> none  [local_step(): back_rows = lax.all_to_all(exp_out, 'ep', 2, 0, tiled=True)]
    unnamed x27 -> x4, local copies, waits for them, and re-layouts: 0.51 us -> 15 us
    select_n x2 -> x0, other arithmetic: 6.32 us -> none  [the longest x1 5.01 us: attention_block(): lat_out = jnp.where(at_pos, lat_new[:, None, :], lat_cache)]
    reshape x1 -> x0, local copies, waits for them, and re-layouts: 6.1 us -> none  [local_step(): exp_out = exp_out.reshape(1, local_experts, ep_size * cap_slots, d_model)]
    all_to_all x1 -> x0, starting transfers between devices: 5.05 us -> none  [local_step(): back_rows = lax.all_to_all(exp_out, 'ep', 2, 0, tiled=True)]
  transfers between devices with their start and end apart: 1 -> 0, of which waited for: 1 -> 0; matrix products, arithmetic and copies ran while one was open for 2% -> 0% of each run, Pallas kernels for 0% -> 0%
where the time goes in v1:
time: 164 us; the launch traced here: 163 us
  Pallas kernels  143 us (87%)
  local copies, waits for them, and re-layouts  19.6 us (12%)
    pallas_call x1, Pallas kernels, moe(): pl.pallas_call(functools.partial(moe_kernel, ep, slots), name='experts',...  113 us
    pallas_call x1, Pallas kernels, attention(): pl.pallas_call(attention_kernel, name='attention', grid_spec=grid_spec, o...  29.7 us
    unnamed x4, local copies, waits for them, and re-layouts  15 us

profile of v1, /device:TPU:112, one launch (start us, length us, event | category | flops | bytes accessed | tf_op | source)
XLA Modules:
  0.0 162.8 jit_solution(3282491599057929760)
XLA Ops:
  0.7 0.6 broadcast_in_dim_tile.3.freq_ref
  1.3 1.3 broadcast_in_dim.10.gain_a_ref
  2.6 1.3 broadcast_in_dim.11.gain_f_ref
  3.9 1.4 copy.22.pos_ref
  5.2 4.8 %copy.23.rope_ref = bf16[128,64,64]{2,1,0:T(8,128)(2,1)} copy(bf16[128,64,64]{0,2,1:T(8,128)(2,1)} %param.21) | data formatting | bytes 2097152 | tf_op args[2]
  10.0 4.3 %copy.24.wkv_hbm = bf16[2048,576]{1,0:T(8,128)(2,1)} copy(bf16[2048,576]{0,1:T(8,128)(2,1)} %param.26) | data formatting | bytes 4718592 | tf_op args[7]
  14.3 29.7 %attention.1 = (bf16[128,64,512]{2,1,0:T(8,128)(2,1)}, bf16[128,64,64]{2,1,0:T(8,128)(2,1)}, bf16[128,2048]{1,0:T(8,128)(2,1)}, bf16[128,2048]{1,0:T(8,128)(2,1)}) custom-call(s32[128]{0:T(128)} %pos_smem.1, bf16[128,2048]{1,0:T(8,128)(2,1)} %x_ref.1, s32[128,1]{1,0:T(8,128)} %copy.22.pos_ref, f32[1,128]{1,0:T(1,128)} %broadcast_in_dim_tile.3.freq_ref, ...), custom_call_target="tpu_custom_call" | custom-call | tf_op jit(solution)/shard_map/attention/pallas_call | solution.py:180
  44.0 112.8 %experts.1 = bf16[128,2048]{1,0:T(8,128)(2,1)} custom-call(bf16[128,2048]{1,0:T(8,128)(2,1)} %get-tuple-element.7.h_in, bf16[128,2048]{1,0:T(8,128)(2,1)} %get-tuple-element.8.resid_ref, s32[6,128]{1,0:T(8,128)} %bitcast.4, bf16[64,2048]{1,0:T(8,128)(2,1)} %bitcast.3, bf16[2048,2816]{1,0:T(8,128)(2,1)} %shg.1, bf16[2048,2816]{1,0:T(8,128)(2,1)} %shu.1, ...), custom_call_target="tpu_custom_call" | custom-call | tf_op jit(solution)/shard_map/experts/pallas_call | solution.py:488
  156.9 4.0 %copy.25 = bf16[128,64,64]{0,2,1:T(8,128)(2,1)} copy(bf16[128,64,64]{2,1,0:T(8,128)(2,1)} %get-tuple-element.13) | data formatting | bytes 2097152
  160.9 1.9 %copy.27 = bf16[128,2048]{1,0:T(8,128)(2,1)} copy(bf16[128,2048]{1,0:T(8,128)(2,1)} %experts.1) | data formatting | bytes 1048576
  (2 shorter events, 0.0 us)

commit v2 on v1

--- a/solution.py
+++ b/solution.py
@@ -1,4 +1,5 @@
 import functools
+import math
 
 import jax
 import jax.numpy as jnp
@@ -15,7 +16,9 @@
 VMEM_LIMIT = 67_043_328
 
 GROUP = 8
+GROUPS = 4
 CHUNK = 256
+BY_SLOT = 512
 
 
 def unit_norm(values):
@@ -32,16 +35,15 @@
 
 
 def attention_kernel(
-    pos_smem, x_ref, pos_ref, freq_ref, gain_a_ref, gain_f_ref, lat_ref, rope_ref,
-    wq_hbm, wkv_hbm, wuk_hbm, wuv_hbm, wo_hbm,
+    pos_smem, x_ref, pos_ref, gain_a_ref, gain_f_ref, lat_ref,
+    rope_hbm, wq_hbm, wkv_hbm, wuk_hbm, wuv_hbm, wo_hbm,
     lat_out, rope_out, resid_ref, h_ref,
-    wq, wkv, wuk_even, wuk_odd, wuv, wo, qc, qr, olat, c_scr, k_scr, heads_scr, sem,
+    wq, wkv, wuk_even, wuk_odd, wuv, wo, rope_in, rope_keys, qc, q_first, q_second, olat, c_scr, pos_scr, heads_scr, s_scr, p_scr, sem,
 ):
     step = pl.program_id(0)
     heads, nope, rank = wuk_hbm.shape
-    rope_dim = rope_ref.shape[-1]
-    rows, d_model = x_ref.shape
-    seq = lat_ref.shape[1]
+    seq, rope_dim, rows = rope_in.shape
+    d_model = x_ref.shape[1]
     pairs = heads // 2
     pair_cols = 2 * (nope + rope_dim)
     per_copy = 2
@@ -55,15 +57,17 @@
     kv_copy = pltpu.make_async_copy(wkv_hbm, wkv, sem.at[copies])
     uv_copy = pltpu.make_async_copy(wuv_hbm, wuv, sem.at[copies + 1])
     wo_copy = pltpu.make_async_copy(wo_hbm, wo, sem.at[copies + 2])
+    rope_copy = pltpu.make_async_copy(rope_hbm, rope_in, sem.at[copies + 3])
 
     def uk_copies(i):
-        even = pltpu.make_async_copy(wuk_hbm.at[2 * i], wuk_even.at[i], sem.at[copies + 3 + 2 * i])
-        odd = pltpu.make_async_copy(wuk_hbm.at[2 * i + 1], wuk_odd.at[i, rope_dim : rope_dim + nope], sem.at[copies + 4 + 2 * i])
+        even = pltpu.make_async_copy(wuk_hbm.at[2 * i], wuk_even.at[i], sem.at[copies + 4 + 2 * i])
+        odd = pltpu.make_async_copy(wuk_hbm.at[2 * i + 1], wuk_odd.at[i, rope_dim : rope_dim + nope], sem.at[copies + 5 + 2 * i])
         return even, odd
 
     @pl.when(step == 0)
     def _():
         kv_copy.start()
+        rope_copy.start()
         for i in range(copies):
             q_copy(i).start()
             for j in range(per_copy):
@@ -74,22 +78,38 @@
         zero = jnp.zeros((pairs, rope_dim, rank), BF16)
         wuk_odd[:, :rope_dim] = zero
         wuk_odd[:, rope_dim + nope :] = zero
-        x_norm = (unit_norm(x_ref[...].astype(F32)) * gain_a_ref[...].astype(F32)).astype(BF16)
-        angle = pos_ref[...].astype(F32) * freq_ref[...]
+        gain = gain_a_ref[...].astype(F32).reshape(1, d_model)
+        x_norm = (unit_norm(x_ref[...].astype(F32)) * gain).astype(BF16)
+        pos_row = pos_ref[...]
+        pos_col = jnp.broadcast_to(pos_row.astype(F32), (rows, rows)).T
+        pos_scr[...] = pos_col
+        lane = lax.broadcasted_iota(jnp.int32, (rows, 2 * rope_dim), 1)
+        power = lax.rem(lane, rope_dim // 2).astype(F32) * (2.0 / rope_dim)
+        angle = pos_col * jnp.exp(power * -math.log(ROPE_BASE))
         cos, sin = jnp.cos(angle), jnp.sin(angle)
-        lane = lax.broadcasted_iota(jnp.int32, (rows, 2 * rope_dim), 1)
         first = lax.rem(lane, rope_dim) < rope_dim // 2
 
         def rope(v):
             ahead = pltpu.roll(v, 2 * rope_dim - rope_dim // 2, 1)
             behind = pltpu.roll(v, rope_dim // 2, 1)
-            return (v * cos + jnp.where(first, -ahead, behind) * sin).astype(BF16)
+            return (v * cos + jnp.where(first, -ahead, behind) * sin).astype(BF16).astype(F32)
 
         kv_copy.wait()
-        kv = mm(x_norm, wkv[...])
+        kv = mm_nt(x_norm, wkv[...])
         c_scr[...] = unit_norm(kv[:, :rank]).astype(BF16).astype(F32)
         k_part = kv[:, rank:]
-        k_scr[...] = rope(jnp.concatenate([k_part, k_part], axis=1)).astype(F32)
+        k_new = rope(jnp.concatenate([k_part, k_part], axis=1)).T[:rope_dim]
+        rope_copy.wait()
+
+        half = seq // 2
+        for j in range(half):
+            both = []
+            for pos in (j, j + half):
+                keys = jnp.where(pos_row == pos, k_new, rope_in[pos].astype(F32))
+                rope_out[pos] = keys.astype(BF16)
+                both.append(keys)
+            rope_keys[pl.ds(j, rows, stride=half), :] = jnp.concatenate(both, axis=0).T
+
         for i in range(pairs):
             if i % per_copy == 0:
                 q_copy(i // per_copy).wait()
@@ -99,32 +119,55 @@
             qc[2 * i] = mm(q[:, :nope], wuk_even[i]).astype(BF16).astype(F32)
             qc[2 * i + 1] = mm(q[:, nope:], wuk_odd[i]).astype(BF16).astype(F32)
             both = jnp.where(lane < rope_dim, q[:, nope : 2 * nope].astype(F32), q[:, 2 * nope :].astype(F32))
-            turned = rope(both).astype(F32)
-            qr[2 * i] = turned
-            qr[2 * i + 1] = pltpu.roll(turned, rope_dim, 1)
-
-    at = pl.ds(pl.multiple_of(step * GROUP, GROUP), GROUP)
-    c_new = c_scr[at, :]
-    k_new = k_scr[at, :rope_dim]
-    slot_lat = lax.broadcasted_iota(jnp.int32, (seq, rank), 0)
-    slot_rope = lax.broadcasted_iota(jnp.int32, (seq, rope_dim), 0)
-    for t in range(GROUP):
-        pos = pos_smem[step * GROUP + t]
-        lat_out[t] = jnp.where(slot_lat == pos, c_new[t : t + 1, :], lat_ref[t].astype(F32)).astype(BF16)
-        rope_out[t] = jnp.where(slot_rope == pos, k_new[t : t + 1, :], rope_ref[t].astype(F32)).astype(BF16)
-    keys = lat_out[...].reshape(GROUP * seq, rank)
-    keys_rope = rope_out[...].reshape(GROUP * seq, rope_dim)
-    q_lat = qc[:, at, :].reshape(heads * GROUP, rank).astype(BF16)
-    q_rope = qr[:, at, :].reshape(heads * GROUP, 2 * rope_dim).astype(BF16)[:, :rope_dim]
-    scores = (mm_nt(q_lat, keys) + mm_nt(q_rope, keys_rope)) * (nope + rope_dim) ** -0.5
+            turned = rope(both)
+            even, odd = jnp.where(lane < rope_dim, turned, 0.0), jnp.where(lane < rope_dim, 0.0, turned)
+            q_first[2 * i] = even
+            q_second[2 * i] = pltpu.roll(even, rope_dim, 1)
+            q_first[2 * i + 1] = pltpu.roll(odd, rope_dim, 1)
+            q_second[2 * i + 1] = odd
+
+    for g in range(GROUPS):
+        at = pl.ds(pl.multiple_of((step * GROUPS + g) * GROUP, GROUP), GROUP)
+        mine = pl.ds(g * GROUP, GROUP)
+        c_new = c_scr[at, :]
+        lat_out[mine] = lat_ref[mine]
+        row = lax.broadcasted_iota(jnp.int32, (16, rank), 0)
+        for t in range(GROUP):
+            pos = pos_smem[(step * GROUPS + g) * GROUP + t]
+            base = pl.multiple_of((pos // 16) * 16, 16)
+            old = lat_ref[g * GROUP + t, pl.ds(base, 16), :].astype(F32)
+            lat_out[g * GROUP + t, pl.ds(base, 16), :] = jnp.where(row == pos - base, c_new[t : t + 1, :], old).astype(BF16)
+    half = seq // 2
     key_id = lax.broadcasted_iota(jnp.int32, (GROUP, GROUP * seq), 1)
-    low = lax.broadcasted_iota(jnp.int32, (GROUP, GROUP * seq), 0) * seq
-    seen = (key_id >= low) & (key_id <= low + pos_ref[at, :])
-    scores = jnp.where(seen[None], scores.reshape(heads, GROUP, GROUP * seq), -jnp.inf)
-    expd = jnp.exp(scores - jnp.max(scores, axis=-1, keepdims=True))
-    prob = (expd / jnp.sum(expd, axis=-1, keepdims=True)).astype(BF16)
-    out = mm(prob.reshape(heads * GROUP, GROUP * seq), keys).astype(BF16).astype(F32)
-    olat[:, at, :] = out.reshape(heads, GROUP, rank)
+    in_half = lax.rem(key_id, GROUP * half)
+    same = in_half // half == lax.broadcasted_iota(jnp.int32, (GROUP, GROUP * seq), 0)
+    key_pos = (lax.rem(in_half, half) + key_id // (GROUP * half) * half).astype(F32)
+
+    def tokens(g):
+        return pl.ds(pl.multiple_of((step * GROUPS + g) * GROUP, GROUP), GROUP)
+
+    def keys_of(g, k):
+        return lat_out[pl.ds(g * GROUP, GROUP), k * half : (k + 1) * half].reshape(GROUP * half, rank)
+
+    for g in range(GROUPS):
+        first_row = pl.multiple_of((step * GROUPS + g) * GROUP * half, GROUP * half)
+        turned_keys = rope_keys[pl.ds(first_row, GROUP * half), :].astype(BF16)
+        q_lat = qc[:, tokens(g), :].reshape(heads * GROUP, rank).astype(BF16)
+        for k, q_part in enumerate((q_first, q_second)):
+            q_rope = q_part[:, tokens(g), :].reshape(heads * GROUP, 2 * rope_dim).astype(BF16)
+            s_scr[g, :, k * GROUP * half : (k + 1) * GROUP * half] = mm_nt(q_lat, keys_of(g, k)) + mm_nt(q_rope, turned_keys)
+    for g in range(GROUPS):
+        seen = same & (key_pos <= jnp.concatenate([pos_scr[tokens(g), :]] * (GROUP * seq // rows), axis=-1))
+        for h in range(0, heads, 4):
+            part = pl.ds(h * GROUP, 4 * GROUP)
+            scores = s_scr[g, part, :].reshape(4, GROUP, GROUP * seq) * (nope + rope_dim) ** -0.5
+            scores = jnp.where(seen[None], scores, -jnp.inf)
+            expd = jnp.exp(scores - jnp.max(scores, axis=-1, keepdims=True))
+            prob = (expd * (1.0 / jnp.sum(expd, axis=-1, keepdims=True))).astype(BF16)
+            p_scr[g, part, :] = prob.reshape(4 * GROUP, GROUP * seq)
+    for g in range(GROUPS):
+        out = mm(p_scr[g], jnp.concatenate([keys_of(g, 0), keys_of(g, 1)], axis=0)).astype(BF16).astype(F32)
+        olat[:, tokens(g), :] = out.reshape(heads, GROUP, rank)
 
     @pl.when(step == pl.num_programs(0) - 1)
     def _():
@@ -137,7 +180,8 @@
         for n in range(0, d_model, piece):
             part = mm(heads_scr[...], wo[:, n : n + piece])
             resid_ref[:, n : n + piece] = (x_ref[:, n : n + piece].astype(F32) + part).astype(BF16)
-        h_ref[...] = (unit_norm(resid_ref[...].astype(F32)) * gain_f_ref[...].astype(F32)).astype(BF16)
+        gain = gain_f_ref[...].astype(F32).reshape(1, d_model)
+        h_ref[...] = (unit_norm(resid_ref[...].astype(F32)) * gain).astype(BF16)
 
 
 def attention(tok_in, lat_cache, rope_cache, tok_pos, attn_gain, w_query, w_kvdown, w_ukey, w_uval, w_out, ffn_gain):
@@ -146,50 +190,53 @@
     rope_dim = rope_cache.shape[-1]
     heads, nope, _ = w_ukey.shape
     v_dim = w_uval.shape[-1]
-    inv_freq = ROPE_BASE ** (-(2.0 * jnp.arange(rope_dim // 2)) / rope_dim)
-    freq = jnp.tile(inv_freq, 4)[None, :]
 
     def const(shape):
         return pl.BlockSpec(shape, lambda g, *_: (0,) * len(shape))
 
     any_spec = pl.BlockSpec(memory_space=pl.ANY)
-    lat_spec = pl.BlockSpec((GROUP, seq, rank), lambda g, *_: (g, 0, 0))
-    rope_spec = pl.BlockSpec((GROUP, seq, rope_dim), lambda g, *_: (g, 0, 0))
+    lat_spec = pl.BlockSpec((GROUPS * GROUP, seq, rank), lambda g, *_: (g, 0, 0))
+    by_token = (seq, rope_dim, rows)
     grid_spec = pltpu.PrefetchScalarGridSpec(
         num_scalar_prefetch=1,
-        grid=(rows // GROUP,),
-        in_specs=[const((rows, d_model)), const((rows, 1)), const((1, 2 * rope_dim)), const((1, d_model)), const((1, d_model)),
-                  lat_spec, rope_spec] + [any_spec] * 5,
-        out_specs=[lat_spec, rope_spec, const((rows, d_model)), const((rows, d_model))],
+        grid=(rows // (GROUPS * GROUP),),
+        in_specs=[const((rows, d_model)), const((1, rows)), const((d_model,)), const((d_model,)), lat_spec] + [any_spec] * 6,
+        out_specs=[lat_spec, const(by_token), const((rows, d_model)), const((rows, d_model))],
         scratch_shapes=[
             pltpu.VMEM(w_query.shape, BF16),
-            pltpu.VMEM(w_kvdown.shape, BF16),
+            pltpu.VMEM(w_kvdown.shape[::-1], BF16),
             pltpu.VMEM((heads // 2, nope, rank), BF16),
             pltpu.VMEM((heads // 2, nope + 2 * rope_dim, rank), BF16),
             pltpu.VMEM(w_uval.shape, BF16),
             pltpu.VMEM(w_out.shape, BF16),
+            pltpu.VMEM(by_token, BF16),
+            pltpu.VMEM((rows * seq // 2, 2 * rope_dim), F32),
             pltpu.VMEM((heads, rows, rank), F32),
+            pltpu.VMEM((heads, rows, 2 * rope_dim), F32),
             pltpu.VMEM((heads, rows, 2 * rope_dim), F32),
             pltpu.VMEM((heads, rows, rank), F32),
             pltpu.VMEM((rows, rank), F32),
-            pltpu.VMEM((rows, 2 * rope_dim), F32),
+            pltpu.VMEM((rows, rows), F32),
             pltpu.VMEM((rows, heads * v_dim), BF16),
-            pltpu.SemaphoreType.DMA((heads // 4 + 3 + heads,)),
+            pltpu.VMEM((GROUPS, heads * GROUP, GROUP * seq), F32),
+            pltpu.VMEM((GROUPS, heads * GROUP, GROUP * seq), BF16),
+            pltpu.SemaphoreType.DMA((heads // 4 + 4 + heads,)),
         ],
     )
-    return pl.pallas_call(
+    lat_out, rope_out, resid, h_norm = pl.pallas_call(
         attention_kernel,
         name="attention",
         grid_spec=grid_spec,
         out_shape=[
             jax.ShapeDtypeStruct(lat_cache.shape, BF16),
-            jax.ShapeDtypeStruct(rope_cache.shape, BF16),
+            jax.ShapeDtypeStruct(by_token, BF16),
             jax.ShapeDtypeStruct((rows, d_model), BF16),
             jax.ShapeDtypeStruct((rows, d_model), BF16),
         ],
         compiler_params=pltpu.CompilerParams(vmem_limit_bytes=VMEM_LIMIT, dimension_semantics=("arbitrary",)),
-    )(tok_pos, tok_in, tok_pos[:, None], freq, attn_gain[None, :], ffn_gain[None, :], lat_cache, rope_cache,
-      w_query, w_kvdown, w_ukey, w_uval, w_out)
+    )(tok_pos, tok_in, tok_pos[None, :], attn_gain, ffn_gain, lat_cache, rope_cache.transpose(1, 2, 0),
+      w_query, w_kvdown.T, w_ukey, w_uval, w_out)
+    return lat_out, rope_out.transpose(2, 0, 1), resid, h_norm
 
 
 def moe_kernel(
@@ -198,7 +245,8 @@
     out_ref,
     wbuf, h_all, w_send, w_all, pick, weigh, comb, x_all, acts, acts_sh, e_buf,
     part, part_peer, from_peer, transit, final, sh_acc,
-    w_sem, b_sem, ag_send, ag_recv, rt_send, rt_recv, rs_send, rs_recv,
+    sl_w, y_even, y_send, slots_in, rank_home, weigh_home, comb_home, sh_first,
+    w_sem, b_sem, ag_send, ag_recv, rt_send, rt_recv, rs_send, rs_recv, sl_sem, sl_send, sl_recv,
 ):
     rows, d_model = h_in.shape
     local, _, ff = exg.shape
@@ -206,7 +254,7 @@
     half = rows // 2
     pair_slots = 2 * slots
     shared_parts = shg.shape[1] // ff
-    chunks = d_model // CHUNK
+    chunks = (d_model - BY_SLOT) // CHUNK
     per_slot = ff // CHUNK
     me = lax.axis_index("ep")
     chip, core = me // 2, lax.rem(me, 2)
@@ -232,7 +280,7 @@
 
     def down_copy(c, k):
         s = lax.rem(c, 2)
-        cols = pl.ds(pl.multiple_of(c * CHUNK, CHUNK), CHUNK)
+        cols = pl.ds(pl.multiple_of(BY_SLOT + c * CHUNK, CHUNK), CHUNK)
         src = exd.at[k, :, cols] if k < local else shd.at[pl.ds((k - local) * ff, ff), cols]
         return pltpu.make_async_copy(src, down_tile(c, k), b_sem.at[s, k])
 
@@ -243,9 +291,17 @@
         for k in range(local + shared_parts):
             down_copy(c, k).start()
 
+    def slot_copy(e, s):
+        return pltpu.make_async_copy(exd.at[e, :, pl.ds(0, BY_SLOT)], sl_w.at[s], sl_sem.at[s])
+
+    def slot_copy_shared(i):
+        return pltpu.make_async_copy(shd.at[pl.ds(i * ff, ff), pl.ds(0, BY_SLOT)], sl_w.at[i % 2], sl_sem.at[i % 2])
+
     for i in range(shared_parts):
         for c in shared_copies(i):
             c.start()
+    for i in range(shared_parts):
+        slot_copy_shared(i).start()
 
     barrier = pltpu.get_barrier_semaphore()
     others = [(dc, oc) for dc in range(chips) for oc in (False, True) if dc or oc]
@@ -328,12 +384,12 @@
         rest = weigh[...].T
         for k in range(3):
             piece = rest.astype(BF16)
-            comb[r, pl.ds(k * 2 * rows, 2 * rows), :] = piece
+            comb[r, k] = piece
             rest = rest - piece.astype(F32)
 
-        @pl.loop(0, d_model // 512)
+        @pl.loop(0, d_model // 1024)
         def _(n):
-            cols = pl.ds(pl.multiple_of(n * 512, 512), 512)
+            cols = pl.ds(pl.multiple_of(n * 1024, 1024), 1024)
             x = mm(pick[...], h_all[r, :, cols]).astype(BF16)
             for e in range(local):
                 x_all[e, pl.ds(r * pair_slots, pair_slots), cols] = x[e * pair_slots : (e + 1) * pair_slots]
@@ -355,6 +411,33 @@
     up(h_in, 1, acts_sh.at[1])
     for c in expert_copies(1):
         c.start()
+    for i in range(shared_parts):
+        slot_copy_shared(i).wait()
+    y = None
+    for i in range(shared_parts):
+        y_i = mm(acts_sh[i], sl_w[i % 2])
+        y = y_i if y is None else y + y_i
+    sh_first[...] = y
+    for e in range(2):
+        slot_copy(e, e).start()
+
+    has = w_send[...] >= 0.0
+    rank_home[...] = jnp.where(has, mm(jnp.where(has, 1.0, 0.0).astype(BF16), tri), -1.0)
+    home_id = lax.broadcasted_iota(jnp.int32, (slots, rows), 0).astype(F32)
+    for r in range(chips):
+        for q in range(2):
+            at = mine(device(r, bool(q)))
+            rank, w = rank_home[at, :], w_send[at, :]
+            for e in range(local):
+                hit = home_id == rank[e : e + 1, :]
+                weigh_home[pl.ds(((r * 2 + q) * local + e) * slots, slots), :] = jnp.where(hit, w[e : e + 1, :], 0.0)
+    for b in range(0, weigh_home.shape[0], 256):
+        rest = weigh_home[b : b + 256, :].T
+        for k in range(3):
+            piece = rest.astype(BF16)
+            comb_home[k, :, b : b + 256] = piece
+            rest = rest - piece.astype(F32)
+
     for i in range(len(others)):
         route_copy(i).wait_recv()
     wait_recv(0)
@@ -372,24 +455,51 @@
     wait_recv(11, 12)
     place(far)
 
-    @pl.loop(0, local)
-    def _(e):
-        for c in expert_copies(e):
-            c.wait()
-        up(x_all.at[e], lax.rem(e, 2), acts.at[e])
-
-        @pl.when(e < local - 2)
-        def _():
-            for c in expert_copies(e + 2):
-                c.start()
-
-        @pl.when(e >= local - 2)
-        def _():
-            start_down(e - (local - 2))
+    def back_copy(i, p):
+        dc, oc = others[i]
+        return remote(y_send.at[dc, int(oc), p], slots_in.at[(chips - dc) % chips, int(oc), p], sl_send.at[i, p], sl_recv.at[i, p], device(dc, oc))
+
+    @pl.loop(0, local // 2)
+    def _(p):
+        for s in range(2):
+            e = 2 * p + s
+            for c in expert_copies(e):
+                c.wait()
+            up(x_all.at[e], s, acts.at[e])
+
+            @pl.when(p < local // 2 - 1)
+            def _():
+                for c in expert_copies(e + 2):
+                    c.start()
+
+            @pl.when(p == local // 2 - 1)
+            def _():
+                start_down(s)
+
+            slot_copy(e, s).wait()
+            y = mm(acts[e], sl_w[s])
+            if s == 0:
+                y_even[...] = y
+
+            @pl.when(p < local // 2 - 1)
+            def _():
+                slot_copy(e + 2, s).start()
+
+            if s == 1:
+                for r in range(chips):
+                    for q in range(2):
+                        at = r * pair_slots + q * slots
+                        both = jnp.concatenate([y_even[at : at + slots, :], y[at : at + slots]], axis=0).astype(BF16)
+                        if r or q:
+                            y_send[r, q, p] = both
+                        else:
+                            slots_in[0, 0, p] = both
+                for i in range(len(others)):
+                    back_copy(i, p).start()
 
     def rs_copy(i, c):
         src, dst, to = (
-            (part_peer.at[c], from_peer.at[c], peer),
+            (part_peer.at[lax.rem(c, 2)], from_peer.at[c], peer),
             (part.at[c, far, top], transit.at[0, c], right),
             (part.at[c, far, low], transit.at[1, c], left),
             (part.at[c, 1, low], final.at[0, c, low], right),
@@ -420,8 +530,9 @@
 
     @pl.loop(0, chunks)
     def _(c):
+        for k in range(local + shared_parts):
+            down_copy(c, k).wait()
         for k in range(local):
-            down_copy(c, k).wait()
             y = mm(acts[k], down_tile(c, k)[...]).astype(BF16)
             for r in range(chips):
                 e_buf[r, k * pair_slots : (k + 1) * pair_slots, :] = y[r * pair_slots : (r + 1) * pair_slots]
@@ -430,16 +541,19 @@
         def _():
             add_peer(c - 1)
 
+        @pl.when(c >= 2)
+        def _():
+            rs_copy(0, c - 2).wait_send()
+
         for r in range(chips):
-            z = mm(comb[r], e_buf[r])
-            z = z[: 2 * rows] + z[2 * rows : 4 * rows] + z[4 * rows :]
+            e_r = e_buf[r]
+            z = mm(comb[r, 0], e_r) + mm(comb[r, 1], e_r) + mm(comb[r, 2], e_r)
             part[c, r] = z[:rows]
-            part_peer[c, r] = z[rows:]
+            part_peer[lax.rem(c, 2), r] = z[rows:]
         rs_copy(0, c).start()
 
         shared = None
         for k in range(local, local + shared_parts):
-            down_copy(c, k).wait()
             y = mm(acts_sh[k - local], down_tile(c, k)[...])
             shared = y if shared is None else shared + y
         sh_acc[c] = shared
@@ -455,10 +569,16 @@
     add_peer(chunks - 1)
     pass_on(chunks - 2)
     pass_on(chunks - 1)
+    for p in range(local // 2):
+        for i in range(len(others)):
+            back_copy(i, p).wait_recv()
+    back_rows = slots_in[...].reshape(ep * local * slots, BY_SLOT)
+    routed = mm(comb_home[0], back_rows) + mm(comb_home[1], back_rows) + mm(comb_home[2], back_rows)
+    out_ref[:, :BY_SLOT] = (resid_ref[:, :BY_SLOT].astype(F32) + sh_first[...] + routed).astype(BF16)
     for c in range(chunks):
         for i in (3, 4, 5, 6):
             rs_copy(i, c).wait_recv()
-        cols = pl.ds(c * CHUNK, CHUNK)
+        cols = pl.ds(BY_SLOT + c * CHUNK, CHUNK)
         routed = part[c, 0] + final[0, c] + final[1, c]
         out_ref[:, cols] = (resid_ref[:, cols].astype(F32) + sh_acc[c] + routed).astype(BF16)
     for i in range(13):
@@ -466,9 +586,15 @@
     for i in range(len(others)):
         route_copy(i).wait_send()
 
+    for p in range(local // 2):
+        for i in range(len(others)):
+            back_copy(i, p).wait_send()
+    for c in range(chunks - 2, chunks):
+        rs_copy(0, c).wait_send()
+
     @pl.loop(0, chunks)
     def _(c):
-        for i in range(7):
+        for i in range(1, 7):
             rs_copy(i, c).wait_send()
 
 
@@ -480,7 +606,7 @@
     chips = ep // 2
     slots = max(2, -(-2 * rows * top_k // num_experts))
     shared_parts = sh_gate.shape[1] // ff
-    chunks = d_model // CHUNK
+    chunks = (d_model - BY_SLOT) // CHUNK
     pair_slots = 2 * slots
     dma = pltpu.SemaphoreType.DMA
     vmem = pl.BlockSpec(memory_space=pltpu.VMEM)
@@ -498,19 +624,28 @@
             pltpu.VMEM((chips, 2, local, rows), F32),
             pltpu.VMEM((local * pair_slots, 2 * rows), BF16),
             pltpu.VMEM((local * pair_slots, 2 * rows), F32),
-            pltpu.VMEM((chips, 6 * rows, local * pair_slots), BF16),
+            pltpu.VMEM((chips, 3, 2 * rows, local * pair_slots), BF16),
             pltpu.VMEM((local, chips * pair_slots, d_model), BF16),
             pltpu.VMEM((local, chips * pair_slots, ff), BF16),
             pltpu.VMEM((shared_parts, rows, ff), BF16),
             pltpu.VMEM((chips, local * pair_slots, CHUNK), BF16),
             pltpu.VMEM((chunks, chips, rows, CHUNK), F32),
-            pltpu.VMEM((chunks, chips, rows, CHUNK), F32),
+            pltpu.VMEM((2, chips, rows, CHUNK), F32),
             pltpu.VMEM((chunks, chips, rows, CHUNK), F32),
             pltpu.VMEM((2, chunks, rows // 2, CHUNK), F32),
             pltpu.VMEM((2, chunks, rows, CHUNK), F32),
             pltpu.VMEM((chunks, rows, CHUNK), F32),
+            pltpu.VMEM((2, ff, BY_SLOT), BF16),
+            pltpu.VMEM((chips * pair_slots, BY_SLOT), F32),
+            pltpu.VMEM((chips, 2, local // 2, pair_slots, BY_SLOT), BF16),
+            pltpu.VMEM((chips, 2, local // 2, pair_slots, BY_SLOT), BF16),
+            pltpu.VMEM((num_experts, rows), F32),
+            pltpu.VMEM((num_experts * slots, rows), F32),
+            pltpu.VMEM((3, rows, num_experts * slots), BF16),
+            pltpu.VMEM((rows, BY_SLOT), F32),
             dma((2, 2)), dma((2, local + shared_parts)),
             dma((13,)), dma((13,)), dma((ep - 1,)), dma((ep - 1,)), dma((7, chunks)), dma((7, chunks)),
+            dma((2,)), dma((ep - 1, local // 2)), dma((ep - 1, local // 2)),
         ],
         compiler_params=pltpu.CompilerParams(vmem_limit_bytes=VMEM_LIMIT, collective_id=0, has_side_effects=True),
     )(h_norm, resid, expert_ids.T, w_router.T, sh_gate, sh_up, sh_down, ex_gate, ex_up, ex_down)

time: 164 us -> 120 us (0.73)
  Pallas kernels: 143 us -> 117 us
  local copies, waits for them, and re-layouts: 19.6 us -> 1.88 us
    pallas_call x1, Pallas kernels: 113 us -> 92.7 us  [moe(): pl.pallas_call(functools.partial(moe_kernel, ep, slots), name='experts',...]
    unnamed x4 -> x1, local copies, waits for them, and re-layouts: 15 us -> 1.88 us
    pallas_call x1, Pallas kernels: 29.7 us -> 24.2 us  [attention(): pl.pallas_call(attention_kernel, name='attention', grid_spec=grid_spec, o...]
    broadcast_in_dim x3 -> x0, local copies, waits for them, and re-layouts: 3.96 us -> none  [the longest x1 1.38 us: attention(): tok_pos[:, None]]
where the time goes in v2:
time: 120 us; the launch traced here: 119 us
  Pallas kernels  117 us (98%)
  local copies, waits for them, and re-layouts  1.88 us (2%)
    pallas_call x1, Pallas kernels, moe(): pl.pallas_call(functools.partial(moe_kernel, ep, slots), name='experts',...  92.7 us
    pallas_call x1, Pallas kernels, attention(): pl.pallas_call(attention_kernel, name='attention', grid_spec=grid_spec, o...  24.2 us

profile of v2, /device:TPU:112, one launch (start us, length us, event | category | flops | bytes accessed | tf_op | source)
XLA Modules:
  0.0 119.4 jit_solution(6080949156020277552)
XLA Ops:
  0.6 24.2 %attention.1 = (bf16[128,64,512]{2,1,0:T(8,128)(2,1)}, bf16[64,64,128]{2,1,0:T(8,128)(2,1)}, bf16[128,2048]{1,0:T(8,128)(2,1)}, bf16[128,2048]{1,0:T(8,128)(2,1)}) custom-call(s32[128]{0:T(128)} %pos_smem.1, bf16[128,2048]{1,0:T(8,128)(2,1)} %x_ref.1, s32[1,128]{1,0:T(1,128)} %bitcast.10, bf16[2048]{0:T(1024)(128)(2,1)} %gain_a_ref.1, ...), custom_call_target="tpu_custom_call" | custom-call | tf_op jit(solution)/shard_map/attention/pallas_call | solution.py:226
  24.9 92.7 %experts.1 = bf16[128,2048]{1,0:T(8,128)(2,1)} custom-call(bf16[128,2048]{1,0:T(8,128)(2,1)} %get-tuple-element.7.h_in, bf16[128,2048]{1,0:T(8,128)(2,1)} %get-tuple-element.8.resid_ref, s32[6,128]{1,0:T(8,128)} %bitcast.9, bf16[64,2048]{1,0:T(8,128)(2,1)} %bitcast.8, bf16[2048,2816]{1,0:T(8,128)(2,1)} %shg.1, bf16[2048,2816]{1,0:T(8,128)(2,1)} %shu.1, ...), custom_call_target="tpu_custom_call" | custom-call | tf_op jit(solution)/shard_map/experts/pallas_call | solution.py:614
  117.5 1.9 %copy.23 = bf16[128,2048]{1,0:T(8,128)(2,1)} copy(bf16[128,2048]{1,0:T(8,128)(2,1)} %experts.1) | data formatting | bytes 1048576

commit v3 on v2

--- a/solution.py
+++ b/solution.py
@@ -18,7 +18,7 @@
 GROUP = 8
 GROUPS = 4
 CHUNK = 256
-BY_SLOT = 512
+BY_SLOT = 768
 
 
 def unit_norm(values):
@@ -35,10 +35,10 @@
 
 
 def attention_kernel(
-    pos_smem, x_ref, pos_ref, gain_a_ref, gain_f_ref, lat_ref,
-    rope_hbm, wq_hbm, wkv_hbm, wuk_hbm, wuv_hbm, wo_hbm,
-    lat_out, rope_out, resid_ref, h_ref,
-    wq, wkv, wuk_even, wuk_odd, wuv, wo, rope_in, rope_keys, qc, q_first, q_second, olat, c_scr, pos_scr, heads_scr, s_scr, p_scr, sem,
+    pos_smem, x_ref, pos_ref, gain_a_ref, gain_f_ref,
+    lat_hbm, rope_hbm, wq_hbm, wkv_hbm, wuk_hbm, wuv_hbm, wo_hbm,
+    lat_out_hbm, rope_out_hbm, resid_ref, h_ref,
+    wq, wkv, wuk_even, wuk_odd, wuv, wo, rope_in, rope_keys, qc, q_first, q_second, olat, c_scr, pos_scr, heads_scr, s_scr, p_scr, lat, rope_out, sem, lat_sem,
 ):
     step = pl.program_id(0)
     heads, nope, rank = wuk_hbm.shape
@@ -58,6 +58,18 @@
     uv_copy = pltpu.make_async_copy(wuv_hbm, wuv, sem.at[copies + 1])
     wo_copy = pltpu.make_async_copy(wo_hbm, wo, sem.at[copies + 2])
     rope_copy = pltpu.make_async_copy(rope_hbm, rope_in, sem.at[copies + 3])
+    rope_back = pltpu.make_async_copy(rope_out, rope_out_hbm, sem.at[copies + 4 + heads])
+    block = GROUPS * GROUP
+    blocks = rows // block
+
+    def lat_copy(b):
+        at = pl.ds(b * block, block)
+        return pltpu.make_async_copy(lat_hbm.at[at], lat.at[at], lat_sem.at[0, b])
+
+    def lat_back(b):
+        at = pl.ds(b * block, block)
+        return pltpu.make_async_copy(lat.at[at], lat_out_hbm.at[at], lat_sem.at[1, b])
+
 
     def uk_copies(i):
         even = pltpu.make_async_copy(wuk_hbm.at[2 * i], wuk_even.at[i], sem.at[copies + 4 + 2 * i])
@@ -73,6 +85,8 @@
             for j in range(per_copy):
                 for c in uk_copies(i * per_copy + j):
                     c.start()
+        for b in range(blocks):
+            lat_copy(b).start()
         uv_copy.start()
         wo_copy.start()
         zero = jnp.zeros((pairs, rope_dim, rank), BF16)
@@ -102,7 +116,8 @@
         rope_copy.wait()
 
         half = seq // 2
-        for j in range(half):
+
+        def turn_keys(j):
             both = []
             for pos in (j, j + half):
                 keys = jnp.where(pos_row == pos, k_new, rope_in[pos].astype(F32))
@@ -113,9 +128,11 @@
         for i in range(pairs):
             if i % per_copy == 0:
                 q_copy(i // per_copy).wait()
-            for c in uk_copies(i):
-                c.wait()
-            q = mm(x_norm, wq[:, i * pair_cols : (i + 1) * pair_cols]).astype(BF16)
+                for k in range(per_copy):
+                    for c in uk_copies(i + k):
+                        c.wait()
+                q_wide = mm(x_norm, wq[:, i * pair_cols : i * pair_cols + wide]).astype(BF16)
+            q = q_wide[:, i % per_copy * pair_cols : (i % per_copy + 1) * pair_cols]
             qc[2 * i] = mm(q[:, :nope], wuk_even[i]).astype(BF16).astype(F32)
             qc[2 * i + 1] = mm(q[:, nope:], wuk_odd[i]).astype(BF16).astype(F32)
             both = jnp.where(lane < rope_dim, q[:, nope : 2 * nope].astype(F32), q[:, 2 * nope :].astype(F32))
@@ -125,18 +142,20 @@
             q_second[2 * i] = pltpu.roll(even, rope_dim, 1)
             q_first[2 * i + 1] = pltpu.roll(odd, rope_dim, 1)
             q_second[2 * i + 1] = odd
-
+            for j in range(i * half // pairs, (i + 1) * half // pairs):
+                turn_keys(j)
+        rope_back.start()
+
+    lat_copy(step).wait()
+    row = lax.broadcasted_iota(jnp.int32, (16, rank), 0)
     for g in range(GROUPS):
-        at = pl.ds(pl.multiple_of((step * GROUPS + g) * GROUP, GROUP), GROUP)
-        mine = pl.ds(g * GROUP, GROUP)
-        c_new = c_scr[at, :]
-        lat_out[mine] = lat_ref[mine]
-        row = lax.broadcasted_iota(jnp.int32, (16, rank), 0)
+        c_new = c_scr[pl.ds(pl.multiple_of((step * GROUPS + g) * GROUP, GROUP), GROUP), :]
         for t in range(GROUP):
-            pos = pos_smem[(step * GROUPS + g) * GROUP + t]
+            token = (step * GROUPS + g) * GROUP + t
+            pos = pos_smem[token]
             base = pl.multiple_of((pos // 16) * 16, 16)
-            old = lat_ref[g * GROUP + t, pl.ds(base, 16), :].astype(F32)
-            lat_out[g * GROUP + t, pl.ds(base, 16), :] = jnp.where(row == pos - base, c_new[t : t + 1, :], old).astype(BF16)
+            old = lat[token, pl.ds(base, 16), :].astype(F32)
+            lat[token, pl.ds(base, 16), :] = jnp.where(row == pos - base, c_new[t : t + 1, :], old).astype(BF16)
     half = seq // 2
     key_id = lax.broadcasted_iota(jnp.int32, (GROUP, GROUP * seq), 1)
     in_half = lax.rem(key_id, GROUP * half)
@@ -147,7 +166,7 @@
         return pl.ds(pl.multiple_of((step * GROUPS + g) * GROUP, GROUP), GROUP)
 
     def keys_of(g, k):
-        return lat_out[pl.ds(g * GROUP, GROUP), k * half : (k + 1) * half].reshape(GROUP * half, rank)
+        return lat[tokens(g), k * half : (k + 1) * half].reshape(GROUP * half, rank)
 
     for g in range(GROUPS):
         first_row = pl.multiple_of((step * GROUPS + g) * GROUP * half, GROUP * half)
@@ -156,6 +175,7 @@
         for k, q_part in enumerate((q_first, q_second)):
             q_rope = q_part[:, tokens(g), :].reshape(heads * GROUP, 2 * rope_dim).astype(BF16)
             s_scr[g, :, k * GROUP * half : (k + 1) * GROUP * half] = mm_nt(q_lat, keys_of(g, k)) + mm_nt(q_rope, turned_keys)
+    lat_back(step).start()
     for g in range(GROUPS):
         seen = same & (key_pos <= jnp.concatenate([pos_scr[tokens(g), :]] * (GROUP * seq // rows), axis=-1))
         for h in range(0, heads, 4):
@@ -182,6 +202,9 @@
             resid_ref[:, n : n + piece] = (x_ref[:, n : n + piece].astype(F32) + part).astype(BF16)
         gain = gain_f_ref[...].astype(F32).reshape(1, d_model)
         h_ref[...] = (unit_norm(resid_ref[...].astype(F32)) * gain).astype(BF16)
+        for b in range(blocks):
+            lat_back(b).wait()
+        rope_back.wait()
 
 
 def attention(tok_in, lat_cache, rope_cache, tok_pos, attn_gain, w_query, w_kvdown, w_ukey, w_uval, w_out, ffn_gain):
@@ -195,13 +218,12 @@
         return pl.BlockSpec(shape, lambda g, *_: (0,) * len(shape))
 
     any_spec = pl.BlockSpec(memory_space=pl.ANY)
-    lat_spec = pl.BlockSpec((GROUPS * GROUP, seq, rank), lambda g, *_: (g, 0, 0))
     by_token = (seq, rope_dim, rows)
     grid_spec = pltpu.PrefetchScalarGridSpec(
         num_scalar_prefetch=1,
         grid=(rows // (GROUPS * GROUP),),
-        in_specs=[const((rows, d_model)), const((1, rows)), const((d_model,)), const((d_model,)), lat_spec] + [any_spec] * 6,
-        out_specs=[lat_spec, const(by_token), const((rows, d_model)), const((rows, d_model))],
+        in_specs=[const((rows, d_model)), const((1, rows)), const((d_model,)), const((d_model,))] + [any_spec] * 7,
+        out_specs=[any_spec, any_spec, const((rows, d_model)), const((rows, d_model))],
         scratch_shapes=[
             pltpu.VMEM(w_query.shape, BF16),
             pltpu.VMEM(w_kvdown.shape[::-1], BF16),
@@ -220,7 +242,10 @@
             pltpu.VMEM((rows, heads * v_dim), BF16),
             pltpu.VMEM((GROUPS, heads * GROUP, GROUP * seq), F32),
             pltpu.VMEM((GROUPS, heads * GROUP, GROUP * seq), BF16),
-            pltpu.SemaphoreType.DMA((heads // 4 + 4 + heads,)),
+            pltpu.VMEM(lat_cache.shape, BF16),
+            pltpu.VMEM(by_token, BF16),
+            pltpu.SemaphoreType.DMA((heads // 4 + 5 + heads,)),
+            pltpu.SemaphoreType.DMA((2, rows // (GROUPS * GROUP))),
         ],
     )
     lat_out, rope_out, resid, h_norm = pl.pallas_call(
@@ -304,7 +329,7 @@
         slot_copy_shared(i).start()
 
     barrier = pltpu.get_barrier_semaphore()
-    others = [(dc, oc) for dc in range(chips) for oc in (False, True) if dc or oc]
+    others = [(dc, oc) for dc in (chips - 2, 1, chips - 1, 0) for oc in (False, True) if dc or oc]
     for dc, oc in others:
         pl.semaphore_signal(barrier, inc=1, device_id={"ep": device(dc, oc)}, device_id_type=pl.DeviceIdType.MESH)
     pl.semaphore_wait(barrier, len(others))

time: 120 us -> 113 us (0.942)
  Pallas kernels: 117 us -> 110 us
    pallas_call x1, Pallas kernels: 24.2 us -> 19.4 us  [attention(): pl.pallas_call(attention_kernel, name='attention', grid_spec=grid_spec, o...]
    pallas_call x1, Pallas kernels: 92.7 us -> 90.6 us  [moe(): pl.pallas_call(functools.partial(moe_kernel, ep, slots), name='experts',...]
where the time goes in v3:
time: 113 us; the launch traced here: 112 us
  Pallas kernels  110 us (97%)
  local copies, waits for them, and re-layouts  1.88 us (2%)
    pallas_call x1, Pallas kernels, moe(): pl.pallas_call(functools.partial(moe_kernel, ep, slots), name='experts',...  90.6 us
    pallas_call x1, Pallas kernels, attention(): pl.pallas_call(attention_kernel, name='attention', grid_spec=grid_spec, o...  19.4 us

profile of v3, /device:TPU:112, one launch (start us, length us, event | category | flops | bytes accessed | tf_op | source)
XLA Modules:
  0.0 112.5 jit_solution(5757353189735917572)
XLA Ops:
  0.6 19.4 %attention.1 = (bf16[128,64,512]{2,1,0:T(8,128)(2,1)}, bf16[64,64,128]{2,1,0:T(8,128)(2,1)}, bf16[128,2048]{1,0:T(8,128)(2,1)}, bf16[128,2048]{1,0:T(8,128)(2,1)}) custom-call(s32[128]{0:T(128)} %pos_smem.1, bf16[128,2048]{1,0:T(8,128)(2,1)} %x_ref.1, s32[1,128]{1,0:T(1,128)} %bitcast.10, bf16[2048]{0:T(1024)(128)(2,1)} %gain_a_ref.1, ...), custom_call_target="tpu_custom_call" | custom-call | tf_op jit(solution)/shard_map/attention/pallas_call | solution.py:251
  20.0 90.6 %experts.1 = bf16[128,2048]{1,0:T(8,128)(2,1)} custom-call(bf16[128,2048]{1,0:T(8,128)(2,1)} %get-tuple-element.7.h_in, bf16[128,2048]{1,0:T(8,128)(2,1)} %get-tuple-element.8.resid_ref, s32[6,128]{1,0:T(8,128)} %bitcast.9, bf16[64,2048]{1,0:T(8,128)(2,1)} %bitcast.8, bf16[2048,2816]{1,0:T(8,128)(2,1)} %shg.1, bf16[2048,2816]{1,0:T(8,128)(2,1)} %shu.1, ...), custom_call_target="tpu_custom_call" | custom-call | tf_op jit(solution)/shard_map/experts/pallas_call | solution.py:639
  110.6 1.9 %copy.23 = bf16[128,2048]{1,0:T(8,128)(2,1)} copy(bf16[128,2048]{1,0:T(8,128)(2,1)} %experts.1) | data formatting | bytes 1048576
